TPU v7x, 256 devices: a whole 4x4x8 slice. The times are simulated.
256 devices in a mesh: blk: 128 (over z_lo, y, x, core), rep: 2 (over z_hi).
Axes of the slice: x: 4, y: 4, z: 8 (z_hi: 2, z_lo: 4; z = z_hi * 4 + z_lo), core: 2. Of those that a mesh axis runs over, the one named last changes fastest.
Arguments:
- load_coef: bfloat16 [256, 2049, 256], P('blk', None, 'rep'), parts along dimension 2, may hold values from -0.29882812 to 0.29882812
- legendre: bfloat16 [256, 2049, 1024], P('blk'), may hold values from -0.125 to 0.125
- slab_orders: int32 [256], replicated, may hold values from 0 to 1023, as said below
- cycle_rows: int32 [1024], replicated, may hold values from 0 to 1023, each once
Outputs:
- potential: bfloat16 [1024, 128, 4096], P('blk', 'rep'), parts along dimension 1
- energy: float32 [128], P('rep'), parts along dimension 0
There are 2 independent parts, one for each index of `rep`. A program takes and returns all parts, laid end to end along the dimension named above; an argument that names none is the same for every part. Nothing has to cross between parts.
Inputs may be any that keep to these rules, and one draw needn't show every extreme that they name: `slab_orders`: values are distinct and below (2048) / 2. `cycle_rows`: each cycle appears once.
All inputs are finite; a program needn't handle non-finite values.
Results may differ from a plain program's by a relative error of at most 0.0055.
Values may be sent and summed in bfloat16 or wider, within the bound.
A program may use at most 128 MiB of HBM per device.

v0:
```python
import math

import jax
import jax.numpy as jnp
from jax import lax
from jax.sharding import Mesh
from jax.sharding import PartitionSpec as P

NLON = 4096
BLK = ("blk_0", "blk_1", "blk_2", "blk_3")


def one_axis_at_a_time(x, axes):
    for axis in axes:
        x = lax.psum(x, axis)
    return x


def basis_rows(frequency):
    coarse_ids = jnp.arange(NLON // 64, dtype=jnp.int32) * 64
    fine_ids = jnp.arange(64, dtype=jnp.int32)
    scale = 2.0 * math.pi / NLON
    coarse_angles = (frequency[:, None] * coarse_ids[None, :] % NLON).astype(jnp.float32) * scale
    fine_angles = (frequency[:, None] * fine_ids[None, :] % NLON).astype(jnp.float32) * scale
    cos_coarse = jnp.cos(coarse_angles)[:, :, None]
    sin_coarse = jnp.sin(coarse_angles)[:, :, None]
    cos_fine = jnp.cos(fine_angles)[:, None, :]
    sin_fine = jnp.sin(fine_angles)[:, None, :]
    cosine = (cos_coarse * cos_fine - sin_coarse * sin_fine).reshape(frequency.shape[0], NLON)
    sine = (sin_coarse * cos_fine + cos_coarse * sin_fine).reshape(frequency.shape[0], NLON)
    factor = jnp.where(frequency == 0, 1.0, 2.0).astype(jnp.float32)[:, None]
    return ((factor * cosine).astype(jnp.bfloat16), (-factor * sine).astype(jnp.bfloat16))


def fourier(received, low_orders, degree):
    cos_lower, sin_lower = basis_rows(low_orders)
    cos_upper, sin_upper = basis_rows(degree - low_orders)
    fourier_basis = jnp.stack([cos_lower, sin_lower, cos_upper, sin_upper], axis=1)
    return jnp.einsum("rnsf,nsk->rfk", received, fourier_basis, preferred_element_type=jnp.float32)


def shards(load_coef, legendre, slab_orders, cycle_rows):
    blocks = lax.axis_size(BLK)
    position = lax.axis_index(BLK)
    pair_count = load_coef.shape[0]
    slab_rows = load_coef.shape[1]
    fields = load_coef.shape[2] // 2
    lat_count = legendre.shape[2]
    degree = slab_rows - 2
    my_orders = lax.dynamic_slice_in_dim(slab_orders, position * pair_count, pair_count)
    row_ids = jnp.arange(slab_rows, dtype=jnp.int32)
    spectra = []
    for pair_index in range(pair_count):
        in_lower = (row_ids < slab_rows - 1 - my_orders[pair_index])[:, None]
        pair_coef = load_coef[pair_index]
        nothing = jnp.zeros_like(pair_coef)
        stacked = jnp.concatenate(
            [jnp.where(in_lower, pair_coef, nothing), jnp.where(in_lower, nothing, pair_coef)],
            axis=1,
        )
        spectra.append(
            lax.dot_general(
                legendre[pair_index],
                stacked,
                (((0,), (0,)), ((), ())),
                preferred_element_type=jnp.float32,
            ).astype(jnp.bfloat16)
        )
    spectra = jnp.stack(spectra, axis=1).reshape(lat_count, pair_count, 4, fields)
    spectra = jnp.take(spectra, cycle_rows, axis=0)
    all_orders = slab_orders.reshape(blocks, pair_count)
    cycle_grid = fourier(
        lax.all_to_all(spectra, BLK, split_axis=0, concat_axis=1, tiled=True),
        low_orders=all_orders.reshape(-1),
        degree=degree,
    )
    partial_energy = jnp.sum(cycle_grid * cycle_grid, axis=(0, 2))
    summed = one_axis_at_a_time(partial_energy, BLK)
    energy = summed / (lat_count * NLON)
    return (cycle_grid.astype(jnp.bfloat16), energy)


def solution(mesh):
    split = Mesh(
        mesh.devices.reshape(4, 4, 4, 2, mesh.shape["rep"]),
        ("blk_0", "blk_1", "blk_2", "blk_3", "rep"),
    )
    in_specs = (P(BLK, None, "rep"), P(BLK, None, None), P(), P())
    out_specs = (P(BLK, "rep", None), P("rep"))
    return jax.shard_map(
        shards, mesh=split, in_specs=in_specs, out_specs=out_specs, check_vma=False
    )
```

profile of v0, /device:TPU:1, one launch (start us, length us, event | category | flops | bytes accessed | tf_op | source)
XLA Modules:
  0.0 158.2 jit_solution(1284161723024664103)
XLA Ops:
  0.6 0.7 fusion.45
  2.0 0.8 dynamic_slice.3
  4.7 3.6 %fusion.52 = (bf16[1,2049,128]{2,0,1:T(2,128)(2,1)S(1)}, bf16[1,2049,128]{2,0,1:T(2,128)(2,1)S(1)}) fusion(bf16[2,2049,128]{2,0,1:T(2,128)(2,1)} %param.4), kind=kLoop, calls=%fused_computation.100 | loop fusion | bytes 2098176 | tf_op jit(solution)/shard_map/slice | solution.py:55
  8.3 17.4 %fusion.51 = (bf16[1,2049,1024]{2,0,1:T(2,128)(2,1)S(1)}, bf16[1,2049,1024]{2,0,1:T(2,128)(2,1)}) fusion(bf16[2,2049,1024]{2,0,1:T(2,128)(2,1)} %param.5), kind=kLoop, calls=%fused_computation.99 | loop fusion | bytes 16785408 | tf_op jit(solution)/shard_map/slice | solution.py:63
  25.7 1.9 %broadcast_select_fusion.2 = (bf16[2049,128]{1,0:T(8,128)(2,1)S(1)}, bf16[2049,128]{1,0:T(8,128)(2,1)S(1)}, bf16[2049,128]{1,0:T(8,128)(2,1)S(1)}, bf16[2049,128]{1,0:T(8,128)(2,1)S(1)}) fusion(pred[2049]{0:T(1024)(128)(4,1)S(1)} %iota_compare_fusion, bf16[1,2049,128]{2,0,1:T(2,128)(2,1)S(1)} %get-tuple-element.9, ...), kind=kLoop, calls=%fused_computation.39 | loop fusion | flops 1049088 | bytes 3151362 | tf_op jit(solution)/shard_map/jit(_where)/select_n | solution.py:58
  27.7 1.5 fusion.11
  29.2 0.7 copy.12
  29.9 4.9 %fusion.12 = bf16[256,1024]{1,0:T(8,128)(2,1)S(1)} fusion(bf16[1,2049,1024]{2,0,1:T(2,128)(2,1)} %get-tuple-element.3, bf16[2049,128]{1,0:T(8,128)(2,1)S(1)} %get-tuple-element.7, bf16[2049,128]{1,0:T(8,128)(2,1)S(1)} %get-tuple-element.6), kind=kOutput, calls=%fused_computation.29 | convolution fusion | flops 1076626432 | bytes 5769728 | tf_op jit(solution)/shard_map/dot_general | solution.py:62
  34.8 0.7 copy.13
  35.6 3.1 %pad_maximum_fusion = bf16[1024,2,4,64]{3,2,1,0:T(4,128)(2,1)} fusion(bf16[1024,1,4,64]{3,2,1,0:T(4,128)(2,1)S(1)} %copy.13, bf16[1024,1,4,64]{3,2,1,0:T(4,128)(2,1)S(1)} %copy.12), kind=kLoop, calls=%fused_computation.24 | loop fusion | flops 524288 | bytes 2097152 | tf_op jit(solution)/shard_map/stack | solution.py:69
  38.6 5.8 %gather_fusion = bf16[1024,2,4,64]{3,2,1,0:T(4,128)(2,1)S(1)} fusion(bf16[1024,2,4,64]{3,2,1,0:T(4,128)(2,1)} %pad_maximum_fusion, s32[1024]{0:T(1024)S(1)} %fusion.45), kind=kCustom, calls=%fused_computation | custom fusion | bytes 2101248 | tf_op jit(solution)/shard_map/jit(_take)/gather | solution.py:70
  44.5 4.5 %broadcast_select_fusion = bf16[1024,2,4,64]{3,2,1,0:T(4,128)(2,1)} fusion(bf16[1024,2,4,64]{3,2,1,0:T(4,128)(2,1)S(1)} %gather_fusion, pred[1024]{0:T(1024)(128)(4,1)S(1)} %compare_and_fusion), kind=kLoop, calls=%fused_computation.27 | loop fusion | flops 524288 | bytes 2098176 | tf_op jit(solution)/shard_map/jit(_take)/select_n | solution.py:70
  49.0 5.1 %reshape.541 = bf16[128,2,2048]{2,1,0:T(2,128)(2,1)} reshape(bf16[1024,2,4,64]{3,2,1,0:T(4,128)(2,1)} %broadcast_select_fusion) | data formatting | bytes 2097152
  54.0 13.8 %all-to-all-start = ((bf16[128,2,2048]{2,1,0:T(2,128)(2,1)}), bf16[128,2,2048]{2,1,0:T(2,128)(2,1)S(1)}, u32[]{:S(2)}, u32[]{:S(2)}) async-start(bf16[128,2,2048]{2,1,0:T(2,128)(2,1)} %reshape.541), calls=%async_computation | async-start | bytes 2097152 | tf_op jit(solution)/shard_map/all_to_all | solution.py:73
  67.9 1.1 fusion.44
  69.0 6.5 %multiply_subtract_fusion = (f32[256,64,64]{0,2,1:T(8,128)}, f32[256,64,64]{0,2,1:T(8,128)}, f32[256,64,64]{0,2,1:T(8,128)}, f32[256,64,64]{0,2,1:T(8,128)}) fusion(f32[256,64]{0,1:T(8,128)S(1)} %get-tuple-element.29, f32[256,64]{0,1:T(8,128)S(1)} %get-tuple-element.30, f32[256,64]{0,1:T(8,128)S(1)} %get-tuple-element.28, ...), kind=kLoop, calls=%fused_computation.19 | loop fusion | flops 12582912 | bytes 17301504 | tf_op jit(solution)/shard_map/sub | solution.py:29
  75.5 5.6 %copy.19 = f32[256,1,4096]{2,0,1:T(8,128)} copy(f32[256,1,4096]{0,2,1:T(8,128)} %bitcast.54) | data formatting | bytes 8388608 | tf_op jit(solution)/shard_map/add | solution.py:30
  81.1 5.6 %copy.18 = f32[256,1,4096]{2,0,1:T(8,128)} copy(f32[256,1,4096]{0,2,1:T(8,128)} %bitcast.53) | data formatting | bytes 8388608 | tf_op jit(solution)/shard_map/sub | solution.py:29
  86.7 5.6 %copy.17 = f32[256,1,4096]{2,0,1:T(8,128)} copy(f32[256,1,4096]{0,2,1:T(8,128)} %bitcast.52) | data formatting | bytes 8388608 | tf_op jit(solution)/shard_map/add | solution.py:30
  92.3 5.6 %copy.16 = f32[256,1,4096]{2,0,1:T(8,128)} copy(f32[256,1,4096]{0,2,1:T(8,128)} %bitcast.51) | data formatting | bytes 8388608 | tf_op jit(solution)/shard_map/sub | solution.py:29
  97.9 4.1 %multiply_convert_fusion = bf16[256,1,4096]{2,0,1:T(8,128)(2,1)} fusion(f32[256,1,4096]{2,0,1:T(8,128)} %copy.19, f32[256]{0:T(256)S(1)} %get-tuple-element.19), kind=kLoop, calls=%fused_computation.16 | loop fusion | flops 2097152 | bytes 6292480 | tf_op jit(solution)/shard_map/convert_element_type | solution.py:32
  102.1 1.8 %multiply_convert_fusion.1 = bf16[256,1,4096]{2,0,1:T(8,128)(2,1)} fusion(f32[256,1,4096]{2,0,1:T(8,128)S(1)} %copy-done.2, f32[256]{0:T(256)S(1)} %get-tuple-element.21), kind=kLoop, calls=%fused_computation.18 | loop fusion | flops 2097152 | bytes 6292480 | tf_op jit(solution)/shard_map/convert_element_type | solution.py:32
  103.9 1.1 copy-done.1
  105.0 1.8 %multiply_convert_fusion.2 = bf16[256,1,4096]{2,0,1:T(8,128)(2,1)} fusion(f32[256,1,4096]{2,0,1:T(8,128)S(1)} %copy-done.1, f32[256]{0:T(256)S(1)} %get-tuple-element.20), kind=kLoop, calls=%fused_computation.20 | loop fusion | flops 2097152 | bytes 6292480 | tf_op jit(solution)/shard_map/convert_element_type | solution.py:32
  106.8 1.8 %multiply_convert_fusion.3 = bf16[256,1,4096]{2,0,1:T(8,128)(2,1)} fusion(f32[256,1,4096]{2,0,1:T(8,128)S(1)} %copy-done, f32[256]{0:T(256)S(1)} %get-tuple-element.18), kind=kLoop, calls=%fused_computation.22 | loop fusion | flops 2097152 | bytes 6292480 | tf_op jit(solution)/shard_map/convert_element_type | solution.py:32
  108.6 1.4 reshape.542
  113.4 7.7 %bitcast_convert_fusion = (bf16[8,64,4096]{2,1,0:T(8,128)(2,1)}, f32[8,64,4096,1]{2,1,3,0:T(8,128)S(1)}) fusion(bf16[256,1,4096]{2,0,1:T(8,128)(2,1)S(1)} %copy-done.3, bf16[256,1,4096]{2,0,1:T(8,128)(2,1)S(1)} %copy-done.4, bf16[256,1,4096]{2,0,1:T(8,128)(2,1)S(1)} %copy-done.5, bf16[256,1,4096]{2,0,1:T(8,128)(2,1)S(1)} %copy-done.6, ...), kind=kOutput, calls=%fused_computation.10 | convolution fusion | flops 4309647360 | bytes 22020096 | tf_op jit(solution)/shard_map/rnsf,nsk->rfk/dot_general | solution.py:39
  121.1 0.8 fusion.7
  121.9 10.3 %psum.28 = f32[64]{0:T(128)S(1)} all-reduce(f32[64]{0:T(128)S(1)} %fusion.7), channel_id=1, replica_groups=mesh['blk_0'=4,'blk_1'=4,'blk_2'=4,'blk_3'=2,'rep'=2] {'blk_0'}, use_global_device_ids=true, to_apply=%region_1.2 | all-reduce | flops 64 | bytes 512 | tf_op jit(solution)/shard_map/psum | solution.py:15
  132.2 8.5 %psum.29 = f32[64]{0:T(128)S(1)} all-reduce(f32[64]{0:T(128)S(1)} %psum.28), channel_id=1, replica_groups=mesh['blk_0'=4,'blk_1'=4,'blk_2'=4,'blk_3'=2,'rep'=2] {'blk_1'}, use_global_device_ids=true, to_apply=%region_2.3 | all-reduce | flops 64 | bytes 512 | tf_op jit(solution)/shard_map/psum | solution.py:15
  140.7 8.4 %psum.30 = f32[64]{0:T(128)S(1)} all-reduce(f32[64]{0:T(128)S(1)} %psum.29), channel_id=1, replica_groups=mesh['blk_0'=4,'blk_1'=4,'blk_2'=4,'blk_3'=2,'rep'=2] {'blk_2'}, use_global_device_ids=true, to_apply=%region_3.4 | all-reduce | flops 64 | bytes 512 | tf_op jit(solution)/shard_map/psum | solution.py:15
  149.1 8.5 %psum.31 = f32[64]{0:T(128)S(1)} all-reduce(f32[64]{0:T(128)S(1)} %psum.30), channel_id=1, replica_groups=mesh['blk_0'=4,'blk_1'=4,'blk_2'=4,'blk_3'=2,'rep'=2] {'blk_3'}, use_global_device_ids=true, to_apply=%region_4.5 | all-reduce | flops 64 | bytes 512 | tf_op jit(solution)/shard_map/psum | solution.py:15
  (26 shorter events, 5.3 us)
Async XLA Ops:
  44.5 23.4 %copy-start.7 = (s32[256]{0:T(256)S(1)}, s32[256]{0:T(256)}, u32[]{:S(2)}) copy-start(s32[256]{0:T(256)} %param.6) | copy-start | bytes 3076
  54.0 54.5 %all-to-all-start = ((bf16[128,2,2048]{2,1,0:T(2,128)(2,1)}), bf16[128,2,2048]{2,1,0:T(2,128)(2,1)S(1)}, u32[]{:S(2)}, u32[]{:S(2)}) async-start(bf16[128,2,2048]{2,1,0:T(2,128)(2,1)} %reshape.541), calls=%async_computation | async-start | bytes 2097152 | tf_op jit(solution)/shard_map/all_to_all | solution.py:73
  97.9 4.1 %copy-start.2 = (f32[256,1,4096]{2,0,1:T(8,128)S(1)}, f32[256,1,4096]{2,0,1:T(8,128)}, u32[]{:S(2)}) copy-start(f32[256,1,4096]{2,0,1:T(8,128)} %copy.18) | copy-start | bytes 12582916
  102.1 2.9 %copy-start.1 = (f32[256,1,4096]{2,0,1:T(8,128)S(1)}, f32[256,1,4096]{2,0,1:T(8,128)}, u32[]{:S(2)}) copy-start(f32[256,1,4096]{2,0,1:T(8,128)} %copy.17) | copy-start | bytes 12582916
  103.9 2.9 %copy-start = (f32[256,1,4096]{2,0,1:T(8,128)S(1)}, f32[256,1,4096]{2,0,1:T(8,128)}, u32[]{:S(2)}) copy-start(f32[256,1,4096]{2,0,1:T(8,128)} %copy.16) | copy-start | bytes 12582916
  109.9 1.6 %copy-start.3 = (bf16[256,1,4096]{2,0,1:T(8,128)(2,1)S(1)}, bf16[256,1,4096]{2,0,1:T(8,128)(2,1)}, u32[]{:S(2)}) copy-start(bf16[256,1,4096]{2,0,1:T(8,128)(2,1)} %multiply_convert_fusion) | copy-start | bytes 6291460
  109.9 2.2 %copy-start.4 = (bf16[256,1,4096]{2,0,1:T(8,128)(2,1)S(1)}, bf16[256,1,4096]{2,0,1:T(8,128)(2,1)}, u32[]{:S(2)}) copy-start(bf16[256,1,4096]{2,0,1:T(8,128)(2,1)} %multiply_convert_fusion.1) | copy-start | bytes 6291460
  109.9 2.8 %copy-start.5 = (bf16[256,1,4096]{2,0,1:T(8,128)(2,1)S(1)}, bf16[256,1,4096]{2,0,1:T(8,128)(2,1)}, u32[]{:S(2)}) copy-start(bf16[256,1,4096]{2,0,1:T(8,128)(2,1)} %multiply_convert_fusion.2) | copy-start | bytes 6291460
  110.0 3.4 %copy-start.6 = (bf16[256,1,4096]{2,0,1:T(8,128)(2,1)S(1)}, bf16[256,1,4096]{2,0,1:T(8,128)(2,1)}, u32[]{:S(2)}) copy-start(bf16[256,1,4096]{2,0,1:T(8,128)(2,1)} %multiply_convert_fusion.3) | copy-start | bytes 6291460
where the time goes:
time: 159 us; the launch traced here: 158 us
  local copies, waits for them, and re-layouts  63.1 us (40%)
  blocking collectives  35.8 us (23%)
  other arithmetic  29.2 us (18%)
  matrix products  14.1 us (9%)
  starting transfers between devices  13.8 us (9%)
  between operations  2.12 us (1%)
    psum x4, blocking collectives, one_axis_at_a_time(): x = lax.psum(x, axis)  35.8 us
    slice x1, local copies, waits for them, and re-layouts, shards(): legendre[pair_index]  17.4 us
    all_to_all x1, starting transfers between devices, shards(): lax.all_to_all(spectra, BLK, split_axis=0, concat_axis=1, tiled=True)  13.8 us
    add x2, local copies, waits for them, and re-layouts, basis_rows(): sin_coarse * cos_fine + cos_coarse * sin_fine  11.2 us
    sub x2, local copies, waits for them, and re-layouts, basis_rows(): cos_coarse * cos_fine - sin_coarse * sin_fine  11.2 us
    unnamed x18, local copies, waits for them, and re-layouts  10.2 us
    dot_general x1, matrix products, fourier(): jnp.einsum('rnsf,nsk->rfk', received, fourier_basis, preferred_element_ty...  7.67 us
    sub x1, other arithmetic, basis_rows(): cos_coarse * cos_fine - sin_coarse * sin_fine  6.49 us
  transfers between devices with their start and end apart: 1, of which 0 were waited for; matrix products, arithmetic and copies ran while one was open for 25% of the time, Pallas kernels for 0%

commit v1 on v0

--- a/solution.py
+++ b/solution.py
@@ -3,17 +3,14 @@
 import jax
 import jax.numpy as jnp
 from jax import lax
-from jax.sharding import Mesh
+from jax.experimental import pallas as pl
+from jax.experimental.pallas import tpu as pltpu
 from jax.sharding import PartitionSpec as P
 
 NLON = 4096
-BLK = ("blk_0", "blk_1", "blk_2", "blk_3")
-
-
-def one_axis_at_a_time(x, axes):
-    for axis in axes:
-        x = lax.psum(x, axis)
-    return x
+BLK = "blk"
+N = 128
+MESH = pl.DeviceIdType.MESH
 
 
 def basis_rows(frequency):
@@ -37,6 +34,56 @@
     cos_upper, sin_upper = basis_rows(degree - low_orders)
     fourier_basis = jnp.stack([cos_lower, sin_lower, cos_upper, sin_upper], axis=1)
     return jnp.einsum("rnsf,nsk->rfk", received, fourier_basis, preferred_element_type=jnp.float32)
+
+
+def exchange_kernel(x_ref, o_ref, send_sem, recv_sem):
+    me = lax.axis_index(BLK)
+    barrier = pltpu.get_barrier_semaphore()
+
+    def greet(step, carry):
+        pl.semaphore_signal(
+            barrier, inc=1, device_id={BLK: (me + step) % N}, device_id_type=MESH
+        )
+        return carry
+
+    lax.fori_loop(1, N, greet, 0)
+    pl.semaphore_wait(barrier, N - 1)
+
+    def send(step, carry):
+        target = (me + (step % 4) * 32 + step // 4) % N
+        pltpu.make_async_remote_copy(
+            src_ref=x_ref.at[target],
+            dst_ref=o_ref.at[me],
+            send_sem=send_sem,
+            recv_sem=recv_sem,
+            device_id={BLK: target},
+            device_id_type=MESH,
+        ).start()
+        return carry
+
+    lax.fori_loop(1, N, send, 0)
+    o_ref[me] = x_ref[me]
+    everything = pltpu.make_async_remote_copy(
+        src_ref=x_ref.at[pl.ds(0, N - 1)],
+        dst_ref=o_ref.at[pl.ds(0, N - 1)],
+        send_sem=send_sem,
+        recv_sem=recv_sem,
+        device_id={BLK: (me + 1) % N},
+        device_id_type=MESH,
+    )
+    everything.wait()
+
+
+def exchange(x):
+    return pl.pallas_call(
+        exchange_kernel,
+        out_shape=jax.ShapeDtypeStruct(x.shape, x.dtype),
+        in_specs=[pl.BlockSpec(memory_space=pltpu.VMEM)],
+        out_specs=pl.BlockSpec(memory_space=pltpu.VMEM),
+        scratch_shapes=[pltpu.SemaphoreType.DMA, pltpu.SemaphoreType.DMA],
+        name="exchange",
+        compiler_params=pltpu.CompilerParams(collective_id=0, has_side_effects=True),
+    )(x)
 
 
 def shards(load_coef, legendre, slab_orders, cycle_rows):
@@ -69,24 +116,20 @@
     spectra = jnp.stack(spectra, axis=1).reshape(lat_count, pair_count, 4, fields)
     spectra = jnp.take(spectra, cycle_rows, axis=0)
     all_orders = slab_orders.reshape(blocks, pair_count)
-    cycle_grid = fourier(
-        lax.all_to_all(spectra, BLK, split_axis=0, concat_axis=1, tiled=True),
-        low_orders=all_orders.reshape(-1),
-        degree=degree,
-    )
+    rows = lat_count // blocks
+    received = exchange(spectra.reshape(blocks, 2 * rows, -1))
+    received = received.reshape(blocks, rows, pair_count, 4, fields)
+    received = received.transpose(1, 0, 2, 3, 4).reshape(rows, blocks * pair_count, 4, fields)
+    cycle_grid = fourier(received, low_orders=all_orders.reshape(-1), degree=degree)
     partial_energy = jnp.sum(cycle_grid * cycle_grid, axis=(0, 2))
-    summed = one_axis_at_a_time(partial_energy, BLK)
+    summed = lax.psum(partial_energy, BLK)
     energy = summed / (lat_count * NLON)
     return (cycle_grid.astype(jnp.bfloat16), energy)
 
 
 def solution(mesh):
-    split = Mesh(
-        mesh.devices.reshape(4, 4, 4, 2, mesh.shape["rep"]),
-        ("blk_0", "blk_1", "blk_2", "blk_3", "rep"),
-    )
     in_specs = (P(BLK, None, "rep"), P(BLK, None, None), P(), P())
     out_specs = (P(BLK, "rep", None), P("rep"))
     return jax.shard_map(
-        shards, mesh=split, in_specs=in_specs, out_specs=out_specs, check_vma=False
+        shards, mesh=mesh, in_specs=in_specs, out_specs=out_specs, check_vma=False
     )

time: 159 us -> 477 us (3.00)
  blocking collectives: 35.8 us -> 333 us
  Pallas kernels: 0 us -> 38.1 us
  starting transfers between devices: 13.8 us -> 0 us
  local copies, waits for them, and re-layouts: 63.1 us -> 56.1 us
    psum x4 -> x1, blocking collectives: 35.8 us -> 333 us  [shards(): summed = lax.psum(partial_energy, BLK)]
    pallas_call x0 -> x1, Pallas kernels: none -> 38.1 us  [exchange(): pl.pallas_call(exchange_kernel, out_shape=jax.ShapeDtypeStruct(x.shape, x...]
    all_to_all x1 -> x0, starting transfers between devices: 13.8 us -> none  [shards(): lax.all_to_all(spectra, BLK, split_axis=0, concat_axis=1, tiled=True)]
    unnamed x18 -> x12, local copies, waits for them, and re-layouts: 10.2 us -> 1.34 us
  transfers between devices with their start and end apart: 1 -> 0, of which waited for: 0 -> 0; matrix products, arithmetic and copies ran while one was open for 25% -> 0% of each run, Pallas kernels for 0% -> 0%
where the time goes in v1:
time: 477 us; the launch traced here: 473 us
  blocking collectives  333 us (70%)
  local copies, waits for them, and re-layouts  56.1 us (12%)
  Pallas kernels  38.1 us (8%)
  other arithmetic  30.1 us (6%)
  matrix products  14.1 us (3%)
    psum x1, blocking collectives, shards(): summed = lax.psum(partial_energy, BLK)  333 us
    pallas_call x1, Pallas kernels, exchange(): pl.pallas_call(exchange_kernel, out_shape=jax.ShapeDtypeStruct(x.shape, x...  38.1 us
    slice x1, local copies, waits for them, and re-layouts, shards(): legendre[pair_index]  13 us
    sub x2, local copies, waits for them, and re-layouts, basis_rows(): cos_coarse * cos_fine - sin_coarse * sin_fine  11.3 us
    add x2, local copies, waits for them, and re-layouts, basis_rows(): sin_coarse * cos_fine + cos_coarse * sin_fine  11.2 us

profile of v1, /device:TPU:1, one launch (start us, length us, event | category | flops | bytes accessed | tf_op | source)
XLA Modules:
  0.0 473.2 jit_solution(17874079537007181945)
XLA Ops:
  0.6 0.8 dynamic_slice.3
  1.4 0.6 fusion.53
  3.3 4.0 fusion.52
  7.3 1.9 broadcast_select_fusion.2
  9.3 13.0 %fusion.51 = (bf16[1,2049,1024]{2,0,1:T(2,128)(2,1)S(1)}, bf16[1,2049,1024]{2,0,1:T(2,128)(2,1)}) fusion(bf16[2,2049,1024]{2,0,1:T(2,128)(2,1)S(1)} %copy-done), kind=kLoop, calls=%fused_computation.98 | loop fusion | bytes 16785408 | tf_op jit(solution)/shard_map/slice | solution.py:110
  22.3 1.5 fusion.11
  23.8 0.7 copy.14
  24.6 4.9 %fusion.12 = bf16[256,1024]{1,0:T(8,128)(2,1)S(1)} fusion(bf16[1,2049,1024]{2,0,1:T(2,128)(2,1)} %get-tuple-element.3, bf16[2049,128]{1,0:T(8,128)(2,1)S(1)} %get-tuple-element.7, bf16[2049,128]{1,0:T(8,128)(2,1)S(1)} %get-tuple-element.6), kind=kOutput, calls=%fused_computation.27 | convolution fusion | flops 1076626432 | bytes 5769728 | tf_op jit(solution)/shard_map/dot_general | solution.py:109
  29.5 0.7 copy.15
  30.2 3.1 pad_maximum_fusion
  33.3 5.8 %gather_fusion = bf16[1024,2,4,64]{3,2,1,0:T(4,128)(2,1)S(1)} fusion(bf16[1024,2,4,64]{3,2,1,0:T(4,128)(2,1)} %pad_maximum_fusion, s32[1024]{0:T(1024)S(1)} %fusion.45), kind=kCustom, calls=%fused_computation | custom fusion | bytes 2101248 | tf_op jit(solution)/shard_map/jit(_take)/gather | solution.py:117
  39.1 1.4 gather.7
  40.8 1.2 broadcast_select_fusion.x_ref
  42.1 38.1 %exchange.1 = bf16[128,16,256]{2,1,0:T(8,128)(2,1)} custom-call(bf16[128,16,256]{2,1,0:T(8,128)(2,1)} %broadcast_select_fusion.x_ref), custom_call_target="tpu_custom_call" | custom-call | tf_op jit(solution)/shard_map/exchange/pallas_call | solution.py:78
  80.1 1.9 copy.16
  82.1 3.0 copy.17
  85.1 1.1 fusion.44
  86.2 6.7 %multiply_subtract_fusion = (f32[256,64,64]{0,2,1:T(8,128)}, f32[256,64,64]{0,2,1:T(8,128)}, f32[256,64,64]{0,2,1:T(8,128)}, f32[256,64,64]{0,2,1:T(8,128)}) fusion(f32[256,64]{0,1:T(8,128)S(1)} %get-tuple-element.29, f32[256,64]{0,1:T(8,128)S(1)} %get-tuple-element.30, f32[256,64]{0,1:T(8,128)S(1)} %get-tuple-element.28, ...), kind=kLoop, calls=%fused_computation.19 | loop fusion | flops 12582912 | bytes 17301504 | tf_op jit(solution)/shard_map/sub | solution.py:26
  92.8 5.7 %copy.21 = f32[256,1,4096]{2,0,1:T(8,128)} copy(f32[256,1,4096]{0,2,1:T(8,128)} %bitcast.54) | data formatting | bytes 8388608 | tf_op jit(solution)/shard_map/add | solution.py:27
  98.5 4.0 multiply_convert_fusion
  102.5 5.7 %copy.20 = f32[256,1,4096]{2,0,1:T(8,128)} copy(f32[256,1,4096]{0,2,1:T(8,128)} %bitcast.53) | data formatting | bytes 8388608 | tf_op jit(solution)/shard_map/sub | solution.py:26
  108.2 4.0 multiply_convert_fusion.1
  112.1 5.6 %copy.19 = f32[256,1,4096]{2,0,1:T(8,128)} copy(f32[256,1,4096]{0,2,1:T(8,128)} %bitcast.52) | data formatting | bytes 8388608 | tf_op jit(solution)/shard_map/add | solution.py:27
  117.7 4.0 multiply_convert_fusion.2
  121.7 5.6 %copy.18 = f32[256,1,4096]{2,0,1:T(8,128)} copy(f32[256,1,4096]{0,2,1:T(8,128)} %bitcast.51) | data formatting | bytes 8388608 | tf_op jit(solution)/shard_map/sub | solution.py:26
  127.3 2.8 multiply_convert_fusion.3
  130.2 0.6 copy-done.2
  130.8 0.6 copy-done.3
  131.4 7.7 %bitcast_convert_fusion = (bf16[8,64,4096]{2,1,0:T(8,128)(2,1)}, f32[8,64,4096,1]{2,1,3,0:T(8,128)S(1)}) fusion(bf16[256,1,4096]{2,0,1:T(8,128)(2,1)S(1)} %copy-done.1, bf16[256,1,4096]{2,0,1:T(8,128)(2,1)S(1)} %copy-done.2, bf16[256,1,4096]{2,0,1:T(8,128)(2,1)S(1)} %copy-done.3, bf16[256,1,4096]{2,0,1:T(8,128)(2,1)S(1)} %multiply_convert_fusion.3, ...), kind=kOutput, calls=%fused_computation.10 | convolution fusion | flops 4309647360 | bytes 22020096 | tf_op jit(solution)/shard_map/rnsf,nsk->rfk/dot_general | solution.py:36
  139.1 0.8 fusion.7
  139.9 332.9 %psum.7 = f32[64]{0:T(128)S(1)} all-reduce(f32[64]{0:T(128)S(1)} %fusion.7), channel_id=1, replica_groups=mesh['blk'=128,'rep'=2] {'blk'}, use_global_device_ids=true, to_apply=%region_1.2 | all-reduce | flops 64 | bytes 512 | tf_op jit(solution)/shard_map/psum | solution.py:125
  472.7 0.5 broadcast_multiply_fusion
  (22 shorter events, 0.4 us)
Async XLA Ops:
  3.3 6.0 %copy-start = (bf16[2,2049,1024]{2,0,1:T(2,128)(2,1)S(1)}, bf16[2,2049,1024]{2,0,1:T(2,128)(2,1)}, u32[]{:S(2)}) copy-start(bf16[2,2049,1024]{2,0,1:T(2,128)(2,1)} %param.5) | copy-start | bytes 25178116
  29.5 3.8 copy-start.4
  42.1 43.0 %copy-start.5 = (s32[256]{0:T(256)S(1)}, s32[256]{0:T(256)}, u32[]{:S(2)}) copy-start(s32[256]{0:T(256)} %param.6) | copy-start | bytes 3076
  127.3 2.9 copy-start.1
  127.3 3.5 copy-start.2
  127.3 4.1 copy-start.3

commit v2 on v0

v2 whole, which is shorter than its diff:
```python
import functools
import math

import jax
import jax.numpy as jnp
from jax import lax
from jax.experimental import pallas as pl
from jax.experimental.pallas import tpu as pltpu
from jax.sharding import PartitionSpec as P

BLK = "blk"
N = 128
NLON = 4096
HALF = NLON // 2
ROWS = 2049
MESH = pl.DeviceIdType.MESH
BF16 = jnp.bfloat16
F32 = jnp.float32


def partner(me, step):
    z, y, x, c = lax.div(me, 32), lax.rem(lax.div(me, 8), 4), lax.rem(lax.div(me, 2), 4), lax.rem(me, 2)
    z = lax.rem(z + lax.rem(step, 4), 4)
    y = lax.rem(y + lax.rem(lax.div(step, 4), 4), 4)
    x = lax.rem(x + lax.rem(lax.div(step, 16), 4), 4)
    c = lax.rem(c + lax.div(step, 64), 2)
    return z * 32 + y * 8 + x * 2 + c


def lanes(shape, dim=1):
    return lax.broadcasted_iota(jnp.int32, shape, dim)


def arrange(group, received, swap, rows_by_source, lhs):
    for q in range(4):
        first = received[group, 32 * q : 32 * q + 16].reshape(256, 128)
        second = received[group, 32 * q + 16 : 32 * q + 32].reshape(256, 128)
        both = jnp.concatenate([first, second], axis=1)
        moved = jnp.dot(swap, both, preferred_element_type=F32).astype(BF16)
        rows_by_source[:, 32 * q : 32 * q + 16, :] = moved[:, :128].reshape(16, 16, 128)
        rows_by_source[:, 32 * q + 16 : 32 * q + 32, :] = moved[:, 128:].reshape(16, 16, 128)
    for row in range(16):
        p, h, i = row // 8, (row // 4) % 2, row % 4
        turned = rows_by_source[row].T
        for part in range(2):
            lhs[h, 64 * i : 64 * i + 64, (2 * p + part) * 128 : (2 * p + part + 1) * 128] = turned[
                64 * part : 64 * part + 64
            ]


def swap_matrix():
    row, col = lanes((256, 256), 0), lanes((256, 256), 1)
    return jnp.where(col == (row % 16) * 16 + row // 16, 1.0, 0.0).astype(BF16)


def exchange_kernel(
    leg_hbm, coef_hbm, orders_hbm, cycles_hbm,
    wave_ref, lhs_ref, basis_ref, energy_ref,
    leg, coef, orders, cycles, order_rows, cycle_cols, pick, coef_lo, coef_hi, spec,
    outgoing, incoming, by_source, lhs_first, esend, erecv,
    load_sem, send_sem, recv_sem, esend_sem, erecv_sem,
):
    me = lax.axis_index(BLK)
    small = [
        pltpu.make_async_copy(cycles_hbm, cycles, load_sem.at[8]),
        pltpu.make_async_copy(orders_hbm, orders, load_sem.at[9]),
        pltpu.make_async_copy(coef_hbm, coef, load_sem.at[10]),
    ]
    for copy in small:
        copy.start()
    big = [pltpu.make_async_copy(leg_hbm.at[:, b], leg.at[b], load_sem.at[b]) for b in range(8)]
    for copy in big:
        copy.start()

    barrier = pltpu.get_barrier_semaphore()

    def greet(step, carry):
        target = lax.rem(me + step, N)
        pl.semaphore_signal(barrier, inc=1, device_id={BLK: target}, device_id_type=MESH)
        return carry

    lax.fori_loop(1, N, greet, 0)

    small[0].wait()
    turned = cycles[...].astype(F32).T
    for b in range(8):
        cycle_cols[128 * b : 128 * b + 128, :] = jnp.broadcast_to(turned[:, b : b + 1], (128, 128))
    lane16 = lanes((16, 128)).astype(F32)

    def fill(t, carry):
        upper = cycle_cols[pl.ds(pl.multiple_of(partner(me, 2 * t) * 8, 8), 8), :]
        lower = cycle_cols[pl.ds(pl.multiple_of(partner(me, 2 * t + 1) * 8, 8), 8), :]
        wanted = jnp.concatenate([upper, lower], axis=0)
        at = pl.ds(pl.multiple_of(t * 16, 16), 16)
        for b in range(8):
            pick[at, 128 * b : 128 * b + 128] = jnp.where(wanted == lane16 + 128.0 * b, 1.0, 0.0).astype(BF16)
        return carry

    lax.fori_loop(0, N // 2, fill, 0)

    small[1].wait()
    turned = orders[...].astype(F32).T
    for b in range(2):
        order_rows[128 * b : 128 * b + 128, :] = jnp.broadcast_to(turned[:, b : b + 1], (128, 128))
    mine = [order_rows[pl.ds(2 * me + p, 1), :].astype(jnp.int32) for p in range(2)]

    small[2].wait()
    flat = coef.reshape(2 * ROWS, 128)

    def split_low(b, carry):
        turned = flat[pl.ds(pl.multiple_of(b * 128, 128), 128), :].T
        index = lanes((1, 128))
        at = pl.ds(pl.multiple_of(b * 128, 128), 128)
        for p in range(2):
            keep = jnp.where(index % 2 == p, 1.0, 0.0).astype(BF16)
            coef_lo[128 * p : 128 * p + 128, at] = turned * keep
        return carry

    def split_high(b, carry):
        turned = flat[pl.ds(pl.multiple_of(b * 128 + 2048, 128), 128), :].T
        index = lanes((1, 128))
        row = 1024 + b * 64 + index // 2
        at = pl.ds(pl.multiple_of(b * 128, 128), 128)
        for p in range(2):
            own = jnp.where(index % 2 == p, 1.0, 0.0)
            lower = jnp.where(row < ROWS - 1 - mine[p], own, 0.0)
            coef_hi[128 * p : 128 * p + 128, at] = turned * lower.astype(BF16)
            coef_hi[256 + 128 * p : 384 + 128 * p, at] = turned * (own - lower).astype(BF16)
        return carry

    lax.fori_loop(0, 16, split_low, 0)
    lax.fori_loop(0, 16, split_high, 0)
    tail = flat[2 * ROWS - 2 : 2 * ROWS, :].astype(F32)
    tail_cols = [jnp.broadcast_to(tail[p : p + 1, :], (128, 128)).T for p in range(2)]
    odd = [mine[p] % 2 == 1 for p in range(2)]

    def synthesize(q, carry):
        for b in range(2):
            pltpu.make_async_copy(leg_hbm.at[:, 0], leg.at[2 * q + b], load_sem.at[2 * q + b]).wait()
        table = [leg.at[2 * q + b].reshape(2 * ROWS, 128) for b in range(2)]
        low = jnp.concatenate([t[0:2048, :] for t in table], axis=1)
        high = jnp.concatenate([t[2048:4096, :] for t in table], axis=1)
        last = jnp.concatenate([t[4096:4098, :] for t in table], axis=1).astype(F32)
        both = jnp.dot(coef_hi[...], high, preferred_element_type=F32)
        lower = both[:256] + jnp.dot(coef_lo[...], low, preferred_element_type=F32)
        upper = both[256:]
        at = pl.ds(pl.multiple_of(q * 256, 256), 256)
        for p in range(2):
            column = jnp.concatenate([tail_cols[p], tail_cols[p]], axis=1)
            lo = lower[128 * p : 128 * p + 128]
            up = upper[128 * p : 128 * p + 128] + column * last[p : p + 1, :]
            is_odd = jnp.concatenate([odd[p], odd[p]], axis=1)
            spec[256 * p : 256 * p + 128, at] = jnp.where(is_odd, up, lo).astype(BF16)
            spec[256 * p + 128 : 256 * p + 256, at] = jnp.where(is_odd, lo, up).astype(BF16)
        return carry

    lax.fori_loop(0, 4, synthesize, 0)

    def permute(q, total):
        rows = pick[pl.ds(pl.multiple_of(q * 256, 256), 256), :]
        moved = lax.dot_general(rows, spec[...], (((1,), (1,)), ((), ())), preferred_element_type=F32)
        moved = moved.reshape(32, 8, 512)
        for g in range(2):
            quarters = [moved[:, 4 * g : 4 * g + 4, 128 * a : 128 * a + 128] for a in range(4)]
            tile = jnp.concatenate(quarters, axis=1).astype(BF16)
            outgoing[g, pl.ds(pl.multiple_of(q * 32, 32), 32)] = tile
        return total + jnp.sum(moved * moved, axis=0)

    squares = lax.fori_loop(0, 4, permute, jnp.zeros((8, 512), F32))

    part = lanes((1, 128)) // 64
    energy = jnp.zeros((1, 128), F32)
    sums = jnp.sum(squares, axis=0, keepdims=True)
    for p in range(2):
        zero_weight = jnp.where(part == 0, 1.0, 0.0)
        weight = jnp.where(mine[p] == 0, zero_weight, 2.0)
        energy += sums[:, 256 * p : 256 * p + 128] * weight
        energy += sums[:, 256 * p + 128 : 256 * p + 256] * 2.0
    energy = (energy + pltpu.roll(energy, 64, 1)) * (1.0 / 1024.0)
    esend[...] = energy
    erecv[me] = energy

    pl.semaphore_wait(barrier, N - 1)

    def send_group(g):
        def send(step, carry):
            target = partner(me, step)
            pltpu.make_async_remote_copy(
                src_ref=outgoing.at[g, step], dst_ref=incoming.at[g, me],
                send_sem=send_sem.at[g], recv_sem=recv_sem.at[g],
                device_id={BLK: target}, device_id_type=MESH,
            ).start()
            return carry

        lax.fori_loop(1, N, send, 0)
        incoming[g, me] = outgoing[g, 0]

    def send_energy(step, carry):
        pltpu.make_async_remote_copy(
            src_ref=esend, dst_ref=erecv.at[me], send_sem=esend_sem, recv_sem=erecv_sem,
            device_id={BLK: partner(me, step)}, device_id_type=MESH,
        ).start()
        return carry

    send_group(0)
    lax.fori_loop(1, N, send_energy, 0)
    send_group(1)

    lane = lanes((128, 128))
    scale = 2.0 * math.pi / NLON

    def build(a, carry):
        p, h = lax.div(a, 2), lax.rem(a, 2)
        m = order_rows[pl.ds(p, N, stride=2), :].astype(jnp.int32)
        m = jnp.where(m % 2 == h, m, ROWS - 2 - m)
        fine = ((m * lane) & (NLON - 1)).astype(F32) * scale
        coarse = ((m * (lane * 128)) & (NLON - 1)).astype(F32) * scale
        factor = jnp.where(m == 0, 1.0, 2.0)
        cos_fine, sin_fine = jnp.cos(fine), jnp.sin(fine)
        cos_coarse, sin_coarse = factor * jnp.cos(coarse), factor * jnp.sin(coarse)
        top = pl.multiple_of(p * 256, 256)
        for b in range(HALF // 128):
            c = jnp.broadcast_to(cos_coarse[:, b : b + 1], (128, 128))
            s = jnp.broadcast_to(sin_coarse[:, b : b + 1], (128, 128))
            at = slice(128 * b, 128 * b + 128)
            basis_ref[h, pl.ds(top, 128), at] = (c * cos_fine - s * sin_fine).astype(BF16)
            basis_ref[h, pl.ds(top + 128, 128), at] = (-(s * cos_fine + c * sin_fine)).astype(BF16)
        return carry

    lax.fori_loop(0, 4, build, 0)
    swap = swap_matrix()

    def arrival(g):
        return pltpu.make_async_remote_copy(
            src_ref=outgoing.at[g, pl.ds(0, N - 1)], dst_ref=incoming.at[g, pl.ds(0, N - 1)],
            send_sem=send_sem.at[g], recv_sem=recv_sem.at[g],
            device_id={BLK: partner(me, 1)}, device_id_type=MESH,
        )

    arrival(0).wait()
    arrange(0, incoming, swap, by_source, lhs_first)

    def stage(k, carry):
        low, high = synthesis(lhs_first, basis_ref, k)
        wave_ref[:, :, pl.ds(pl.multiple_of(k * 256, 256), 256)] = low
        wave_ref[:, :, pl.ds(pl.multiple_of(k * 256 + HALF, 256), 256)] = high
        return carry

    lax.fori_loop(0, HALF // 256, stage, 0)

    pltpu.make_async_remote_copy(
        src_ref=erecv.at[pl.ds(0, N - 1)], dst_ref=erecv.at[pl.ds(0, N - 1)],
        send_sem=esend_sem, recv_sem=erecv_sem,
        device_id={BLK: partner(me, 1)}, device_id_type=MESH,
    ).wait()
    energy_ref[...] = jnp.sum(erecv[...], axis=0)

    arrival(1).wait()
    arrange(1, incoming, swap, by_source, lhs_ref)


def synthesis(lhs, basis, k):
    at = pl.ds(pl.multiple_of(k * 256, 256), 256)
    even = jnp.dot(lhs[0], basis[0, :, at], preferred_element_type=F32)
    odd = jnp.dot(lhs[1], basis[1, :, at], preferred_element_type=F32)
    return (even + odd).astype(BF16).reshape(4, 64, 256), (even - odd).astype(BF16).reshape(4, 64, 256)


def finish_kernel(wave_ref, lhs_ref, basis_ref, energy_in, out_ref, energy_ref, second, sem):
    first = pltpu.make_async_copy(wave_ref, out_ref.at[0:4], sem.at[0])
    first.start()
    energy_ref[...] = energy_in[:, :64]
    copies = []
    for k in range(HALF // 256):
        low, high = synthesis(lhs_ref, basis_ref, k)
        second[:, :, 256 * k : 256 * k + 256] = low
        second[:, :, HALF + 256 * k : HALF + 256 * k + 256] = high
        if k % 2 == 1:
            for j, start in enumerate((256 * (k - 1), HALF + 256 * (k - 1))):
                at = pl.ds(start, 512)
                copy = pltpu.make_async_copy(second.at[:, :, at], out_ref.at[4:8, :, at], sem.at[1 + (k // 2) * 2 + j])
                copy.start()
                copies.append(copy)
    first.wait()
    for copy in copies:
        copy.wait()


def shards(load_coef, legendre, slab_orders, cycle_rows):
    legendre = legendre.reshape(2, ROWS, 8, 128).transpose(1, 2, 0, 3)
    load_coef = load_coef.transpose(1, 0, 2)
    hbm = pl.BlockSpec(memory_space=pltpu.HBM)
    vmem = pl.BlockSpec(memory_space=pltpu.VMEM)
    wave, lhs, basis, energy = pl.pallas_call(
        exchange_kernel,
        out_shape=(
            jax.ShapeDtypeStruct((4, 64, NLON), BF16),
            jax.ShapeDtypeStruct((2, 256, 512), BF16),
            jax.ShapeDtypeStruct((2, 512, HALF), BF16),
            jax.ShapeDtypeStruct((1, 128), F32),
        ),
        in_specs=[hbm] * 4,
        out_specs=(vmem,) * 4,
        scratch_shapes=[
            pltpu.VMEM((8, ROWS, 2, 128), BF16),
            pltpu.VMEM((ROWS, 2, 128), BF16),
            pltpu.VMEM((2, 128), jnp.int32),
            pltpu.VMEM((8, 128), jnp.int32),
            pltpu.VMEM((256, 128), F32),
            pltpu.VMEM((1024, 128), F32),
            pltpu.VMEM((1024, 1024), BF16),
            pltpu.VMEM((256, 2048), BF16),
            pltpu.VMEM((512, 2048), BF16),
            pltpu.VMEM((512, 1024), BF16),
            pltpu.VMEM((2, N, 16, 128), BF16),
            pltpu.VMEM((2, N, 16, 128), BF16),
            pltpu.VMEM((16, N, 128), BF16),
            pltpu.VMEM((2, 256, 512), BF16),
            pltpu.VMEM((1, 128), F32),
            pltpu.VMEM((N, 1, 128), F32),
            pltpu.SemaphoreType.DMA((11,)),
            pltpu.SemaphoreType.DMA((2,)),
            pltpu.SemaphoreType.DMA((2,)),
            pltpu.SemaphoreType.DMA,
            pltpu.SemaphoreType.DMA,
        ],
        name="exchange",
        compiler_params=pltpu.CompilerParams(
            collective_id=0, has_side_effects=True, vmem_limit_bytes=40 * 2**20
        ),
    )(legendre, load_coef, slab_orders.reshape(2, 128), cycle_rows.reshape(8, 128))
    potential, energy = pl.pallas_call(
        finish_kernel,
        out_shape=(
            jax.ShapeDtypeStruct((8, 64, NLON), BF16),
            jax.ShapeDtypeStruct((1, 64), F32),
        ),
        in_specs=[vmem] * 4,
        out_specs=(hbm, vmem),
        scratch_shapes=[pltpu.VMEM((4, 64, NLON), BF16), pltpu.SemaphoreType.DMA((9,))],
        name="finish",
        compiler_params=pltpu.CompilerParams(vmem_limit_bytes=40 * 2**20),
    )(wave, lhs, basis, energy)
    return potential, energy.reshape(64)


def solution(mesh):
    in_specs = (P(BLK, None, "rep"), P(BLK, None, None), P(), P())
    out_specs = (P(BLK, "rep", None), P("rep"))
    return jax.shard_map(shards, mesh=mesh, in_specs=in_specs, out_specs=out_specs, check_vma=False)
```

time: 159 us -> 55.8 us (0.35)
  local copies, waits for them, and re-layouts: 63.1 us -> 2.58 us
  Pallas kernels: 0 us -> 52.4 us
  blocking collectives: 35.8 us -> 0 us
  other arithmetic: 29.2 us -> 0 us
  matrix products: 14.1 us -> 0 us
  starting transfers between devices: 13.8 us -> 0 us
    pallas_call x0 -> x2, Pallas kernels: none -> 52.4 us  [the longest x1 49.6 us: shards(): pl.pallas_call(exchange_kernel, out_shape=(jax.ShapeDtypeStruct((4, 64, N...]
    psum x4 -> x0, blocking collectives: 35.8 us -> none  [one_axis_at_a_time(): x = lax.psum(x, axis)]
    slice x3 -> x0, local copies, waits for them, and re-layouts: 21.6 us -> none  [the longest x1 17.4 us: shards(): legendre[pair_index]]
    dot_general x3 -> x0, matrix products: 14.1 us -> none  [the longest x1 7.67 us: fourier(): jnp.einsum('rnsf,nsk->rfk', received, fourier_basis, preferred_element_ty...]
    all_to_all x1 -> x0, starting transfers between devices: 13.8 us -> none  [shards(): lax.all_to_all(spectra, BLK, split_axis=0, concat_axis=1, tiled=True)]
    add x2 -> x0, local copies, waits for them, and re-layouts: 11.2 us -> none  [basis_rows(): sin_coarse * cos_fine + cos_coarse * sin_fine]
    sub x2 -> x0, local copies, waits for them, and re-layouts: 11.2 us -> none  [basis_rows(): cos_coarse * cos_fine - sin_coarse * sin_fine]
    convert_element_type x4 -> x0, other arithmetic: 9.44 us -> none  [the longest x2 5.88 us: basis_rows(): (-factor * sine).astype(jnp.bfloat16)]
  transfers between devices with their start and end apart: 1 -> 0, of which waited for: 0 -> 0; matrix products, arithmetic and copies ran while one was open for 25% -> 0% of each run, Pallas kernels for 0% -> 0%
where the time goes in v2:
time: 55.8 us; the launch traced here: 55.6 us
  Pallas kernels  52.4 us (94%)
  local copies, waits for them, and re-layouts  2.58 us (5%)
  between operations  0.65 us (1%)
    pallas_call x1, Pallas kernels, shards(): pl.pallas_call(exchange_kernel, out_shape=(jax.ShapeDtypeStruct((4, 64, N...  49.6 us
    pallas_call x1, Pallas kernels, shards(): pl.pallas_call(finish_kernel, out_shape=(jax.ShapeDtypeStruct((8, 64, NLO...  2.77 us
    unnamed x6, local copies, waits for them, and re-layouts  2.58 us

profile of v2, /device:TPU:1, one launch (start us, length us, event | category | flops | bytes accessed | tf_op | source)
XLA Modules:
  0.0 55.6 jit_solution(18154564191057913087)
XLA Ops:
  0.6 0.0 copy-start
  0.6 1.2 %copy-done = bf16[2,2049,128]{2,0,1:T(2,128)(2,1)S(1)} copy-done((bf16[2,2049,128]{2,0,1:T(2,128)(2,1)S(1)}, bf16[2,2049,128]{2,0,1:T(2,128)(2,1)}, u32[]{:S(2)}) %copy-start) | copy-done | bytes 1049112
  1.9 0.0 copy-start.1
  1.9 0.7 %copy-done.1 = s32[1024]{0:T(1024)S(1)} copy-done((s32[1024]{0:T(1024)S(1)}, s32[1024]{0:T(1024)}, u32[]{:S(2)}) %copy-start.1) | copy-done | bytes 4120
  2.5 0.0 copy-start.2
  2.5 0.7 %copy-done.2 = s32[256]{0:T(256)S(1)} copy-done((s32[256]{0:T(256)S(1)}, s32[256]{0:T(256)}, u32[]{:S(2)}) %copy-start.2) | copy-done | bytes 1048
  3.2 49.6 %exchange.1 = (bf16[4,64,4096]{2,1,0:T(8,128)(2,1)S(1)}, bf16[2,256,512]{2,1,0:T(8,128)(2,1)S(1)}, bf16[2,512,2048]{2,1,0:T(8,128)(2,1)S(1)}, f32[1,128]{1,0:T(1,128)S(1)}) custom-call(bf16[2049,8,2,128]{3,2,1,0:T(2,128)(2,1)} %bitcast.10, bf16[2049,2,128]{2,1,0:T(2,128)(2,1)S(1)} %bitcast.7, s32[2,128]{1,0:T(2,128)S(1)} %bitcast.9, s32[8,128]{1,0:T(8,128)S(1)} %bitcast.8), custom_call_target="tpu_custom_call" | custom-call | tf_op jit(solution)/shard_map/exchange/pallas_call | solution.py:294
  52.9 2.8 %finish.1 = (bf16[8,64,4096]{2,1,0:T(8,128)(2,1)}, f32[1,64]{1,0:T(1,128)}) custom-call(bf16[4,64,4096]{2,1,0:T(8,128)(2,1)S(1)} %get-tuple-element.8.wave_ref, bf16[2,256,512]{2,1,0:T(8,128)(2,1)S(1)} %get-tuple-element.9.lhs_ref, bf16[2,512,2048]{2,1,0:T(8,128)(2,1)S(1)} %get-tuple-element.10.basis_ref, f32[1,128]{1,0:T(1,128)S(1)} %get-tuple-element.11.energy_in), custom_call_target="tpu_custom_call" | custom-call | tf_op jit(solution)/shard_map/finish/pallas_call | solution.py:332
Async XLA Ops:
  0.6 1.2 %copy-start = (bf16[2,2049,128]{2,0,1:T(2,128)(2,1)S(1)}, bf16[2,2049,128]{2,0,1:T(2,128)(2,1)}, u32[]{:S(2)}) copy-start(bf16[2,2049,128]{2,0,1:T(2,128)(2,1)} %param.4) | copy-start | bytes 3147268
  1.9 0.7 %copy-start.1 = (s32[1024]{0:T(1024)S(1)}, s32[1024]{0:T(1024)}, u32[]{:S(2)}) copy-start(s32[1024]{0:T(1024)} %param.7) | copy-start | bytes 12292
  2.5 0.7 %copy-start.2 = (s32[256]{0:T(256)S(1)}, s32[256]{0:T(256)}, u32[]{:S(2)}) copy-start(s32[256]{0:T(256)} %param.6) | copy-start | bytes 3076

commit v3 on v2

v3 whole, which is shorter than its diff:
```python
import functools
import math

import jax
import jax.numpy as jnp
from jax import lax
from jax.experimental import pallas as pl
from jax.experimental.pallas import tpu as pltpu
from jax.sharding import PartitionSpec as P

BLK = "blk"
N = 128
NLON = 4096
HALF = NLON // 2
ROWS = 2049
MESH = pl.DeviceIdType.MESH
BF16 = jnp.bfloat16
F32 = jnp.float32


def plane(me, u):
    y, x, c = lax.rem(lax.div(me, 8), 4), lax.rem(lax.div(me, 2), 4), lax.rem(me, 2)
    y = lax.rem(y + lax.rem(u, 4), 4)
    x = lax.rem(x + lax.rem(lax.div(u, 4), 4), 4)
    c = lax.rem(c + lax.div(u, 16), 2)
    return y * 8 + x * 2 + c


def lanes(shape, dim=1):
    return lax.broadcasted_iota(jnp.int32, shape, dim)


def arrange(group, received, swap, rows_by_source, lhs):
    for q in range(4):
        first = received[group, 32 * q : 32 * q + 16].reshape(256, 128)
        second = received[group, 32 * q + 16 : 32 * q + 32].reshape(256, 128)
        both = jnp.concatenate([first, second], axis=1)
        moved = jnp.dot(swap, both, preferred_element_type=F32).astype(BF16)
        rows_by_source[:, 32 * q : 32 * q + 16, :] = moved[:, :128].reshape(16, 16, 128)
        rows_by_source[:, 32 * q + 16 : 32 * q + 32, :] = moved[:, 128:].reshape(16, 16, 128)
    for row in range(16):
        p, h, i = row // 8, (row // 4) % 2, row % 4
        turned = rows_by_source[row].T
        for part in range(2):
            lhs[h, 2 * p + part, 64 * i : 64 * i + 64, :] = turned[64 * part : 64 * part + 64]


def wide(blocks):
    return jnp.concatenate([blocks[b] for b in range(blocks.shape[0])], axis=1)


def swap_matrix():
    row, col = lanes((256, 256), 0), lanes((256, 256), 1)
    return jnp.where(col == (row % 16) * 16 + row // 16, 1.0, 0.0).astype(BF16)


def own_orders(order_rows, me):
    return [order_rows[pl.ds(2 * me + p, 1), :].astype(jnp.int32) for p in range(2)]


def exchange_kernel(
    leg_hbm, coef_hbm, orders_hbm, cycles_hbm,
    wave_ref, lhs_ref, basis_ref, energy_ref,
    leg, coef, orders, cycles, order_rows, pick, coef_lo, coef_hi, spec,
    outgoing, incoming, by_source, lhs_first, esend, erecv,
    load_sem, send_sem, recv_sem, esend_sem, erecv_sem,
):
    me = lax.axis_index(BLK)
    small = [
        pltpu.make_async_copy(cycles_hbm, cycles, load_sem.at[8]),
        pltpu.make_async_copy(orders_hbm, orders, load_sem.at[9]),
        pltpu.make_async_copy(coef_hbm, coef, load_sem.at[10]),
    ]
    for copy in small:
        copy.start()
    big = [
        pltpu.make_async_copy(leg_hbm.at[:, b], leg.at[b], load_sem.at[b]) for b in range(8)
    ]
    for copy in big:
        copy.start()

    barrier = pltpu.get_barrier_semaphore()

    def to_all(act):
        def quad(u, first):
            base = plane(me, u)
            for d in range(first, 4):
                act(base + 32 * lax.rem(lax.div(me, 32) + d, 4))

        def later(u, carry):
            quad(u, 0)
            return carry

        quad(0, 1)
        lax.fori_loop(1, 32, later, 0)

    to_all(lambda target: pl.semaphore_signal(barrier, inc=1, device_id={BLK: target}, device_id_type=MESH))
    small[0].wait()
    turned = cycles[...].astype(F32).T
    high = jnp.floor(turned * (1.0 / 128.0))
    low = turned - 128.0 * high
    lane = lanes((128, 128)).astype(F32).astype(BF16)
    none = jnp.zeros((128, 128), BF16)
    for r in range(8):
        block = jnp.broadcast_to(high[:, r : r + 1], (128, 128)).astype(BF16)
        place = jnp.broadcast_to(low[:, r : r + 1], (128, 128)).astype(BF16)
        ones = jnp.where(place == lane, jnp.ones_like(none), none)
        for b in range(8):
            pick[b, 128 * r : 128 * r + 128, :] = jnp.where(
                block == jnp.full((128, 128), b, BF16), ones, none
            )

    small[1].wait()
    turned = orders[...].astype(F32).T
    for b in range(2):
        order_rows[128 * b : 128 * b + 128, :] = jnp.broadcast_to(turned[:, b : b + 1], (128, 128))
    mine = own_orders(order_rows, me)

    small[2].wait()
    flat = coef.reshape(2 * ROWS, 128)
    index = lanes((1, 128))
    own = [jnp.where(index % 2 == p, 1.0, 0.0) for p in range(2)]
    for b in range(32):
        turned = flat[128 * b : 128 * b + 128, :].T
        for p in range(2):
            if b < 16:
                coef_lo[b, 128 * p : 128 * p + 128, :] = turned * own[p].astype(BF16)
            else:
                lower = jnp.where(64 * b + index // 2 < ROWS - 1 - mine[p], own[p], 0.0)
                coef_hi[b - 16, 128 * p : 128 * p + 128, :] = turned * lower.astype(BF16)
                coef_hi[b - 16, 256 + 128 * p : 384 + 128 * p, :] = turned * (own[p] - lower).astype(BF16)
    tail = flat[2 * ROWS - 2 : 2 * ROWS, :].astype(F32)
    tail_cols = [jnp.broadcast_to(tail[p : p + 1, :], (128, 128)).T for p in range(2)]
    odd = [mine[p] % 2 == 1 for p in range(2)]

    def synthesize(q, carry):
        for b in range(2):
            pltpu.make_async_copy(leg_hbm.at[:, 0], leg.at[2 * q + b], load_sem.at[2 * q + b]).wait()
        table = [leg.at[2 * q + b].reshape(2 * ROWS, 128) for b in range(2)]
        low = jnp.concatenate([t[0:2048, :] for t in table], axis=1)
        high = jnp.concatenate([t[2048:4096, :] for t in table], axis=1)
        last = jnp.concatenate([t[4096:4098, :] for t in table], axis=1).astype(F32)
        both = jnp.dot(wide(coef_hi), high, preferred_element_type=F32)
        lower = both[:256] + jnp.dot(wide(coef_lo), low, preferred_element_type=F32)
        upper = both[256:]
        for p in range(2):
            column = jnp.concatenate([tail_cols[p]] * 2, axis=1)
            lo = lower[128 * p : 128 * p + 128]
            up = upper[128 * p : 128 * p + 128] + column * last[p : p + 1, :]
            is_odd = jnp.concatenate([odd[p]] * 2, axis=1)
            even, other = jnp.where(is_odd, up, lo).astype(BF16), jnp.where(is_odd, lo, up).astype(BF16)
            for b in range(2):
                spec[2 * q + b, 256 * p : 256 * p + 128, :] = even[:, 128 * b : 128 * b + 128]
                spec[2 * q + b, 256 * p + 128 : 256 * p + 256, :] = other[:, 128 * b : 128 * b + 128]
        return carry

    lax.fori_loop(0, 4, synthesize, 0)

    def send_one(g, target):
        pltpu.make_async_remote_copy(
            src_ref=outgoing.at[g, target], dst_ref=incoming.at[g, me],
            send_sem=send_sem.at[g], recv_sem=recv_sem.at[g],
            device_id={BLK: target}, device_id_type=MESH,
        ).start()

    squares = jnp.zeros((8, 512), F32)
    for d in (2, 3, 1, 0):
        z = lax.rem(lax.div(me, 32) + d, 4)
        at = pl.ds(pl.multiple_of(z * 256, 256), 256)
        rows = jnp.concatenate([pick[b, at, :] for b in range(8)], axis=1)
        moved = lax.dot_general(rows, wide(spec), (((1,), (1,)), ((), ())), preferred_element_type=F32)
        moved = moved.reshape(32, 8, 512)
        for g in range(2):
            quarters = [moved[:, 4 * g : 4 * g + 4, 128 * a : 128 * a + 128] for a in range(4)]
            tile = jnp.concatenate(quarters, axis=1).astype(BF16)
            outgoing[g, pl.ds(pl.multiple_of(z * 32, 32), 32)] = tile
        squares += jnp.sum(moved * moved, axis=0)
        if d == 2:
            pl.semaphore_wait(barrier, N - 1)

        def plane_sends(u, carry):
            send_one(0, plane(me, u) + 32 * z)
            return carry

        lax.fori_loop(0 if d else 1, 32, plane_sends, 0)
    incoming[0, me] = outgoing[0, me]

    part = lanes((1, 128)) // 64
    energy = jnp.zeros((1, 128), F32)
    sums = jnp.sum(squares, axis=0, keepdims=True)
    for p in range(2):
        zero_weight = jnp.where(part == 0, 1.0, 0.0)
        weight = jnp.where(mine[p] == 0, zero_weight, 2.0)
        energy += sums[:, 256 * p : 256 * p + 128] * weight
        energy += sums[:, 256 * p + 128 : 256 * p + 256] * 2.0
    energy = (energy + pltpu.roll(energy, 64, 1)) * (1.0 / 1024.0)
    esend[...] = energy
    erecv[me] = energy

    def send_energy(target):
        pltpu.make_async_remote_copy(
            src_ref=esend, dst_ref=erecv.at[me], send_sem=esend_sem, recv_sem=erecv_sem,
            device_id={BLK: target}, device_id_type=MESH,
        ).start()

    to_all(send_energy)
    to_all(functools.partial(send_one, 1))
    incoming[1, me] = outgoing[1, me]

    lane = lanes((128, 128))
    scale = 2.0 * math.pi / NLON

    def build(a, carry):
        p, h = lax.div(a, 2), lax.rem(a, 2)
        m = order_rows[pl.ds(p, N, stride=2), :].astype(jnp.int32)
        m = jnp.where(m % 2 == h, m, ROWS - 2 - m)
        fine = ((m * lane) & (NLON - 1)).astype(F32) * scale
        coarse = ((m * (lane * 128)) & (NLON - 1)).astype(F32) * scale
        factor = jnp.where(m == 0, 1.0, 2.0)
        cos_fine, sin_fine = jnp.cos(fine), jnp.sin(fine)
        cos_coarse, sin_coarse = factor * jnp.cos(coarse), factor * jnp.sin(coarse)
        top = pl.multiple_of(p * 256, 256)
        for b in range(HALF // 128):
            c = jnp.broadcast_to(cos_coarse[:, b : b + 1], (128, 128))
            s = jnp.broadcast_to(sin_coarse[:, b : b + 1], (128, 128))
            basis_ref[h, b, pl.ds(top, 128), :] = (c * cos_fine - s * sin_fine).astype(BF16)
            basis_ref[h, b, pl.ds(top + 128, 128), :] = (-(s * cos_fine + c * sin_fine)).astype(BF16)
        return carry

    lax.fori_loop(0, 4, build, 0)
    swap = swap_matrix()

    def arrival(g):
        return pltpu.make_async_remote_copy(
            src_ref=outgoing.at[g, pl.ds(0, N - 1)], dst_ref=incoming.at[g, pl.ds(0, N - 1)],
            send_sem=send_sem.at[g], recv_sem=recv_sem.at[g],
            device_id={BLK: lax.rem(me + 1, N)}, device_id_type=MESH,
        )

    arrival(0).wait()
    arrange(0, incoming, swap, by_source, lhs_first)

    def stage(k, carry):
        low, high = synthesis(lhs_first, basis_ref, k)
        wave_ref[:, :, pl.ds(pl.multiple_of(k * 256, 256), 256)] = low
        wave_ref[:, :, pl.ds(pl.multiple_of(k * 256 + HALF, 256), 256)] = high
        return carry

    lax.fori_loop(0, HALF // 256, stage, 0)

    pltpu.make_async_remote_copy(
        src_ref=erecv.at[pl.ds(0, N - 1)], dst_ref=erecv.at[pl.ds(0, N - 1)],
        send_sem=esend_sem, recv_sem=erecv_sem,
        device_id={BLK: lax.rem(me + 1, N)}, device_id_type=MESH,
    ).wait()
    energy_ref[...] = jnp.sum(erecv[...], axis=0)

    arrival(1).wait()
    arrange(1, incoming, swap, by_source, lhs_ref)


def synthesis(lhs, basis, k):
    even, odd = (
        jnp.dot(
            wide(lhs.at[h]),
            jnp.concatenate([basis[h, 2 * k], basis[h, 2 * k + 1]], axis=1),
            preferred_element_type=F32,
        )
        for h in range(2)
    )
    return (even + odd).astype(BF16).reshape(4, 64, 256), (even - odd).astype(BF16).reshape(4, 64, 256)


def finish_kernel(wave_ref, lhs_ref, basis_ref, energy_in, out_ref, energy_ref, second, sem):
    first = pltpu.make_async_copy(wave_ref, out_ref.at[0:4], sem.at[0])
    first.start()
    energy_ref[...] = energy_in[:, :64]
    copies = []
    for k in range(HALF // 256):
        low, high = synthesis(lhs_ref, basis_ref, k)
        second[:, :, 256 * k : 256 * k + 256] = low
        second[:, :, HALF + 256 * k : HALF + 256 * k + 256] = high
        if k % 2 == 1:
            for j, start in enumerate((256 * (k - 1), HALF + 256 * (k - 1))):
                at = pl.ds(start, 512)
                copy = pltpu.make_async_copy(second.at[:, :, at], out_ref.at[4:8, :, at], sem.at[1 + (k // 2) * 2 + j])
                copy.start()
                copies.append(copy)
    first.wait()
    for copy in copies:
        copy.wait()


def shards(load_coef, legendre, slab_orders, cycle_rows):
    legendre = legendre.reshape(2, ROWS, 8, 128).transpose(1, 2, 0, 3)
    load_coef = load_coef.transpose(1, 0, 2)
    hbm = pl.BlockSpec(memory_space=pltpu.HBM)
    vmem = pl.BlockSpec(memory_space=pltpu.VMEM)
    operands = (legendre, load_coef, slab_orders.reshape(2, 128), cycle_rows.reshape(8, 128))
    wave, lhs, basis, energy = pl.pallas_call(
        exchange_kernel,
        out_shape=(
            jax.ShapeDtypeStruct((4, 64, NLON), BF16),
            jax.ShapeDtypeStruct((2, 4, 256, 128), BF16),
            jax.ShapeDtypeStruct((2, HALF // 128, 512, 128), BF16),
            jax.ShapeDtypeStruct((1, 128), F32),
        ),
        in_specs=[hbm] * 4,
        out_specs=(vmem,) * 4,
        scratch_shapes=[
            pltpu.VMEM((8, ROWS, 2, 128), BF16),
            pltpu.VMEM((ROWS, 2, 128), BF16),
            pltpu.VMEM((2, 128), jnp.int32),
            pltpu.VMEM((8, 128), jnp.int32),
            pltpu.VMEM((256, 128), F32),
            pltpu.VMEM((8, 1024, 128), BF16),
            pltpu.VMEM((16, 256, 128), BF16),
            pltpu.VMEM((16, 512, 128), BF16),
            pltpu.VMEM((8, 512, 128), BF16),
            pltpu.VMEM((2, N, 16, 128), BF16),
            pltpu.VMEM((2, N, 16, 128), BF16),
            pltpu.VMEM((16, N, 128), BF16),
            pltpu.VMEM((2, 4, 256, 128), BF16),
            pltpu.VMEM((1, 128), F32),
            pltpu.VMEM((N, 1, 128), F32),
            pltpu.SemaphoreType.DMA((11,)),
            pltpu.SemaphoreType.DMA((2,)),
            pltpu.SemaphoreType.DMA((2,)),
            pltpu.SemaphoreType.DMA,
            pltpu.SemaphoreType.DMA,
        ],
        name="exchange",
        compiler_params=pltpu.CompilerParams(
            collective_id=0, has_side_effects=True, vmem_limit_bytes=40 * 2**20
        ),
    )(*[pltpu.with_memory_space_constraint(value, pltpu.HBM) for value in operands])
    potential, energy = pl.pallas_call(
        finish_kernel,
        out_shape=(
            jax.ShapeDtypeStruct((8, 64, NLON), BF16),
            jax.ShapeDtypeStruct((1, 64), F32),
        ),
        in_specs=[vmem] * 4,
        out_specs=(hbm, vmem),
        scratch_shapes=[pltpu.VMEM((4, 64, NLON), BF16), pltpu.SemaphoreType.DMA((9,))],
        name="finish",
        compiler_params=pltpu.CompilerParams(vmem_limit_bytes=24 * 2**20),
    )(wave, lhs, basis, energy)
    return potential, energy.reshape(64)


def solution(mesh):
    in_specs = (P(BLK, None, "rep"), P(BLK, None, None), P(), P())
    out_specs = (P(BLK, "rep", None), P("rep"))
    return jax.shard_map(shards, mesh=mesh, in_specs=in_specs, out_specs=out_specs, check_vma=False)
```

time: 55.8 us -> 46.5 us (0.83)
  Pallas kernels: 52.4 us -> 45.8 us
  local copies, waits for them, and re-layouts: 2.58 us -> 0 us
    pallas_call x1, Pallas kernels: 49.6 us -> 42.7 us  [shards(): pl.pallas_call(exchange_kernel, out_shape=(jax.ShapeDtypeStruct((4, 64, N...]
    unnamed x6 -> x0, local copies, waits for them, and re-layouts: 2.58 us -> none
where the time goes in v3:
time: 46.5 us; the launch traced here: 46.4 us
  Pallas kernels  45.8 us (98%)
  between operations  0.64 us (1%)
    pallas_call x1, Pallas kernels, shards(): pl.pallas_call(exchange_kernel, out_shape=(jax.ShapeDtypeStruct((4, 64, N...  42.7 us
    pallas_call x1, Pallas kernels, shards(): pl.pallas_call(finish_kernel, out_shape=(jax.ShapeDtypeStruct((8, 64, NLO...  3.1 us

profile of v3, /device:TPU:1, one launch (start us, length us, event | category | flops | bytes accessed | tf_op | source)
XLA Modules:
  0.0 46.4 jit_solution(7666881255177826025)
XLA Ops:
  0.6 42.7 %exchange.1 = (bf16[4,64,4096]{2,1,0:T(8,128)(2,1)S(1)}, bf16[2,4,256,128]{3,2,1,0:T(8,128)(2,1)S(1)}, bf16[2,16,512,128]{3,2,1,0:T(8,128)(2,1)S(1)}, f32[1,128]{1,0:T(1,128)S(1)}) custom-call(bf16[2049,8,2,128]{3,2,1,0:T(2,128)(2,1)} %bitcast.7, bf16[2049,2,128]{2,1,0:T(2,128)(2,1)} %bitcast.8, s32[2,128]{1,0:T(2,128)} %bitcast.10, s32[8,128]{1,0:T(8,128)} %bitcast.9), custom_call_target="tpu_custom_call" | custom-call | tf_op jit(solution)/shard_map/exchange/pallas_call | solution.py:300
  43.3 3.1 %finish.1 = (bf16[8,64,4096]{2,1,0:T(8,128)(2,1)}, f32[1,64]{1,0:T(1,128)}) custom-call(bf16[4,64,4096]{2,1,0:T(8,128)(2,1)S(1)} %get-tuple-element.8.wave_ref, bf16[2,4,256,128]{3,2,1,0:T(8,128)(2,1)S(1)} %get-tuple-element.9.lhs_ref, bf16[2,16,512,128]{3,2,1,0:T(8,128)(2,1)S(1)} %get-tuple-element.10.basis_ref, f32[1,128]{1,0:T(1,128)S(1)} %get-tuple-element.11.energy_in), custom_call_target="tpu_custom_call" | custom-call | tf_op jit(solution)/shard_map/finish/pallas_call | solution.py:337

commit v4 on v3

--- a/solution.py
+++ b/solution.py
@@ -62,7 +62,7 @@
     leg_hbm, coef_hbm, orders_hbm, cycles_hbm,
     wave_ref, lhs_ref, basis_ref, energy_ref,
     leg, coef, orders, cycles, order_rows, pick, coef_lo, coef_hi, spec,
-    outgoing, incoming, by_source, lhs_first, esend, erecv,
+    outgoing, incoming, by_source, lhs_first, esend, ecolumn, eplane,
     load_sem, send_sem, recv_sem, esend_sem, erecv_sem,
 ):
     me = lax.axis_index(BLK)
@@ -95,21 +95,6 @@
         lax.fori_loop(1, 32, later, 0)
 
     to_all(lambda target: pl.semaphore_signal(barrier, inc=1, device_id={BLK: target}, device_id_type=MESH))
-    small[0].wait()
-    turned = cycles[...].astype(F32).T
-    high = jnp.floor(turned * (1.0 / 128.0))
-    low = turned - 128.0 * high
-    lane = lanes((128, 128)).astype(F32).astype(BF16)
-    none = jnp.zeros((128, 128), BF16)
-    for r in range(8):
-        block = jnp.broadcast_to(high[:, r : r + 1], (128, 128)).astype(BF16)
-        place = jnp.broadcast_to(low[:, r : r + 1], (128, 128)).astype(BF16)
-        ones = jnp.where(place == lane, jnp.ones_like(none), none)
-        for b in range(8):
-            pick[b, 128 * r : 128 * r + 128, :] = jnp.where(
-                block == jnp.full((128, 128), b, BF16), ones, none
-            )
-
     small[1].wait()
     turned = orders[...].astype(F32).T
     for b in range(2):
@@ -132,6 +117,21 @@
     tail = flat[2 * ROWS - 2 : 2 * ROWS, :].astype(F32)
     tail_cols = [jnp.broadcast_to(tail[p : p + 1, :], (128, 128)).T for p in range(2)]
     odd = [mine[p] % 2 == 1 for p in range(2)]
+
+    small[0].wait()
+    lane = lanes((128, 128)).astype(F32).astype(BF16)
+    none = jnp.zeros((128, 128), BF16)
+    one = jnp.ones((128, 128), BF16)
+
+    def fill(r):
+        wanted = jnp.broadcast_to(cycles[pl.ds(r, 1), :].astype(F32), (128, 128)).T
+        high = jnp.floor(wanted * (1.0 / 128.0))
+        ones = jnp.where((wanted - 128.0 * high).astype(BF16) == lane, one, none)
+        block = high.astype(BF16)
+        for b in range(8):
+            pick[b, pl.ds(pl.multiple_of(r * 128, 128), 128), :] = jnp.where(
+                block == jnp.full((128, 128), b, BF16), ones, none
+            )
 
     def synthesize(q, carry):
         for b in range(2):
@@ -152,6 +152,8 @@
             for b in range(2):
                 spec[2 * q + b, 256 * p : 256 * p + 128, :] = even[:, 128 * b : 128 * b + 128]
                 spec[2 * q + b, 256 * p + 128 : 256 * p + 256, :] = other[:, 128 * b : 128 * b + 128]
+        for j in range(2):
+            fill(2 * q + j)
         return carry
 
     lax.fori_loop(0, 4, synthesize, 0)
@@ -194,16 +196,25 @@
         energy += sums[:, 256 * p : 256 * p + 128] * weight
         energy += sums[:, 256 * p + 128 : 256 * p + 256] * 2.0
     energy = (energy + pltpu.roll(energy, 64, 1)) * (1.0 / 1024.0)
-    esend[...] = energy
-    erecv[me] = energy
-
-    def send_energy(target):
+    mine_z, mine_u = lax.div(me, 32), lax.rem(me, 32)
+    esend[0] = energy
+    ecolumn[mine_z] = energy
+
+    def send_energy(stage, target, slot):
         pltpu.make_async_remote_copy(
-            src_ref=esend, dst_ref=erecv.at[me], send_sem=esend_sem, recv_sem=erecv_sem,
+            src_ref=esend.at[stage], dst_ref=slot, send_sem=esend_sem.at[stage], recv_sem=erecv_sem.at[stage],
             device_id={BLK: target}, device_id_type=MESH,
         ).start()
 
-    to_all(send_energy)
+    def energy_arrival(stage, slots, count):
+        pltpu.make_async_remote_copy(
+            src_ref=slots.at[pl.ds(0, count)], dst_ref=slots.at[pl.ds(0, count)],
+            send_sem=esend_sem.at[stage], recv_sem=erecv_sem.at[stage],
+            device_id={BLK: lax.rem(me + 1, N)}, device_id_type=MESH,
+        ).wait()
+
+    for d in range(1, 4):
+        send_energy(0, mine_u + 32 * lax.rem(mine_z + d, 4), ecolumn.at[mine_z])
     to_all(functools.partial(send_one, 1))
     incoming[1, me] = outgoing[1, me]
 
@@ -237,6 +248,11 @@
             device_id={BLK: lax.rem(me + 1, N)}, device_id_type=MESH,
         )
 
+    energy_arrival(0, ecolumn, 3)
+    partial = jnp.sum(ecolumn[...], axis=0)
+    esend[1] = partial
+    eplane[mine_u] = partial
+
     arrival(0).wait()
     arrange(0, incoming, swap, by_source, lhs_first)
 
@@ -246,15 +262,14 @@
         wave_ref[:, :, pl.ds(pl.multiple_of(k * 256 + HALF, 256), 256)] = high
         return carry
 
+    def plane_energy(u, carry):
+        send_energy(1, plane(me, u) + 32 * mine_z, eplane.at[mine_u])
+        return carry
+
+    lax.fori_loop(1, 32, plane_energy, 0)
     lax.fori_loop(0, HALF // 256, stage, 0)
-
-    pltpu.make_async_remote_copy(
-        src_ref=erecv.at[pl.ds(0, N - 1)], dst_ref=erecv.at[pl.ds(0, N - 1)],
-        send_sem=esend_sem, recv_sem=erecv_sem,
-        device_id={BLK: lax.rem(me + 1, N)}, device_id_type=MESH,
-    ).wait()
-    energy_ref[...] = jnp.sum(erecv[...], axis=0)
-
+    energy_arrival(1, eplane, 31)
+    energy_ref[...] = jnp.sum(eplane[...], axis=0)
     arrival(1).wait()
     arrange(1, incoming, swap, by_source, lhs_ref)
 
@@ -275,20 +290,25 @@
     first = pltpu.make_async_copy(wave_ref, out_ref.at[0:4], sem.at[0])
     first.start()
     energy_ref[...] = energy_in[:, :64]
-    copies = []
-    for k in range(HALF // 256):
-        low, high = synthesis(lhs_ref, basis_ref, k)
-        second[:, :, 256 * k : 256 * k + 256] = low
-        second[:, :, HALF + 256 * k : HALF + 256 * k + 256] = high
-        if k % 2 == 1:
-            for j, start in enumerate((256 * (k - 1), HALF + 256 * (k - 1))):
-                at = pl.ds(start, 512)
-                copy = pltpu.make_async_copy(second.at[:, :, at], out_ref.at[4:8, :, at], sem.at[1 + (k // 2) * 2 + j])
-                copy.start()
-                copies.append(copy)
+
+    def store(k, half):
+        at = pl.ds(pl.multiple_of(k * 512 + HALF * half, 512), 512)
+        return pltpu.make_async_copy(second.at[:, :, at], out_ref.at[4:8, :, at], sem.at[1 + 2 * k + half])
+
+    def stage(k, carry):
+        for j in range(2):
+            low, high = synthesis(lhs_ref, basis_ref, 2 * k + j)
+            second[:, :, pl.ds(pl.multiple_of(k * 512 + 256 * j, 256), 256)] = low
+            second[:, :, pl.ds(pl.multiple_of(k * 512 + 256 * j + HALF, 256), 256)] = high
+        store(k, 0).start()
+        store(k, 1).start()
+        return carry
+
+    lax.fori_loop(0, 4, stage, 0)
     first.wait()
-    for copy in copies:
-        copy.wait()
+    for k in range(4):
+        store(k, 0).wait()
+        store(k, 1).wait()
 
 
 def shards(load_coef, legendre, slab_orders, cycle_rows):
@@ -321,13 +341,14 @@
             pltpu.VMEM((2, N, 16, 128), BF16),
             pltpu.VMEM((16, N, 128), BF16),
             pltpu.VMEM((2, 4, 256, 128), BF16),
-            pltpu.VMEM((1, 128), F32),
-            pltpu.VMEM((N, 1, 128), F32),
+            pltpu.VMEM((2, 1, 128), F32),
+            pltpu.VMEM((4, 1, 128), F32),
+            pltpu.VMEM((32, 1, 128), F32),
             pltpu.SemaphoreType.DMA((11,)),
             pltpu.SemaphoreType.DMA((2,)),
             pltpu.SemaphoreType.DMA((2,)),
-            pltpu.SemaphoreType.DMA,
-            pltpu.SemaphoreType.DMA,
+            pltpu.SemaphoreType.DMA((2,)),
+            pltpu.SemaphoreType.DMA((2,)),
         ],
         name="exchange",
         compiler_params=pltpu.CompilerParams(

time: 46.5 us -> 45.1 us (0.970)
  Pallas kernels: 45.8 us -> 44.4 us
    pallas_call x1, Pallas kernels: 42.7 us -> 41.1 us  [shards(): pl.pallas_call(exchange_kernel, out_shape=(jax.ShapeDtypeStruct((4, 64, N...]
where the time goes in v4:
time: 45.1 us; the launch traced here: 45 us
  Pallas kernels  44.4 us (98%)
  between operations  0.64 us (1%)
    pallas_call x1, Pallas kernels, shards(): pl.pallas_call(exchange_kernel, out_shape=(jax.ShapeDtypeStruct((4, 64, N...  41.1 us
    pallas_call x1, Pallas kernels, shards(): pl.pallas_call(finish_kernel, out_shape=(jax.ShapeDtypeStruct((8, 64, NLO...  3.24 us

profile of v4, /device:TPU:1, one launch (start us, length us, event | category | flops | bytes accessed | tf_op | source)
XLA Modules:
  0.0 45.0 jit_solution(10978605939464446542)
XLA Ops:
  0.6 41.1 %exchange.1 = (bf16[4,64,4096]{2,1,0:T(8,128)(2,1)S(1)}, bf16[2,4,256,128]{3,2,1,0:T(8,128)(2,1)S(1)}, bf16[2,16,512,128]{3,2,1,0:T(8,128)(2,1)S(1)}, f32[1,128]{1,0:T(1,128)S(1)}) custom-call(bf16[2049,8,2,128]{3,2,1,0:T(2,128)(2,1)} %bitcast.7, bf16[2049,2,128]{2,1,0:T(2,128)(2,1)} %bitcast.8, s32[2,128]{1,0:T(2,128)} %bitcast.10, s32[8,128]{1,0:T(8,128)} %bitcast.9), custom_call_target="tpu_custom_call" | custom-call | tf_op jit(solution)/shard_map/exchange/pallas_call | solution.py:320
  41.8 3.2 %finish.1 = (bf16[8,64,4096]{2,1,0:T(8,128)(2,1)}, f32[1,64]{1,0:T(1,128)}) custom-call(bf16[4,64,4096]{2,1,0:T(8,128)(2,1)S(1)} %get-tuple-element.8.wave_ref, bf16[2,4,256,128]{3,2,1,0:T(8,128)(2,1)S(1)} %get-tuple-element.9.lhs_ref, bf16[2,16,512,128]{3,2,1,0:T(8,128)(2,1)S(1)} %get-tuple-element.10.basis_ref, f32[1,128]{1,0:T(1,128)S(1)} %get-tuple-element.11.energy_in), custom_call_target="tpu_custom_call" | custom-call | tf_op jit(solution)/shard_map/finish/pallas_call | solution.py:358

commit v5 on v4

--- a/solution.py
+++ b/solution.py
@@ -104,16 +104,15 @@
     small[2].wait()
     flat = coef.reshape(2 * ROWS, 128)
     index = lanes((1, 128))
-    own = [jnp.where(index % 2 == p, 1.0, 0.0) for p in range(2)]
-    for b in range(32):
-        turned = flat[128 * b : 128 * b + 128, :].T
-        for p in range(2):
-            if b < 16:
-                coef_lo[b, 128 * p : 128 * p + 128, :] = turned * own[p].astype(BF16)
+    for p in range(2):
+        for b in range(16):
+            turned = flat[pl.ds(256 * b + p, 128, stride=2), :].T
+            if b < 8:
+                coef_lo[p, b] = turned
             else:
-                lower = jnp.where(64 * b + index // 2 < ROWS - 1 - mine[p], own[p], 0.0)
-                coef_hi[b - 16, 128 * p : 128 * p + 128, :] = turned * lower.astype(BF16)
-                coef_hi[b - 16, 256 + 128 * p : 384 + 128 * p, :] = turned * (own[p] - lower).astype(BF16)
+                lower = jnp.where(128 * b + index < ROWS - 1 - mine[p], 1.0, 0.0)
+                coef_hi[p, b - 8, 0:128, :] = turned * lower.astype(BF16)
+                coef_hi[p, b - 8, 128:256, :] = turned * (1.0 - lower).astype(BF16)
     tail = flat[2 * ROWS - 2 : 2 * ROWS, :].astype(F32)
     tail_cols = [jnp.broadcast_to(tail[p : p + 1, :], (128, 128)).T for p in range(2)]
     odd = [mine[p] % 2 == 1 for p in range(2)]
@@ -134,29 +133,27 @@
             )
 
     def synthesize(q, carry):
-        for b in range(2):
-            pltpu.make_async_copy(leg_hbm.at[:, 0], leg.at[2 * q + b], load_sem.at[2 * q + b]).wait()
-        table = [leg.at[2 * q + b].reshape(2 * ROWS, 128) for b in range(2)]
-        low = jnp.concatenate([t[0:2048, :] for t in table], axis=1)
-        high = jnp.concatenate([t[2048:4096, :] for t in table], axis=1)
+        for b in range(4):
+            pltpu.make_async_copy(leg_hbm.at[:, 0], leg.at[4 * q + b], load_sem.at[4 * q + b]).wait()
+        table = [leg.at[4 * q + b].reshape(2 * ROWS, 128) for b in range(4)]
         last = jnp.concatenate([t[4096:4098, :] for t in table], axis=1).astype(F32)
-        both = jnp.dot(wide(coef_hi), high, preferred_element_type=F32)
-        lower = both[:256] + jnp.dot(wide(coef_lo), low, preferred_element_type=F32)
-        upper = both[256:]
         for p in range(2):
-            column = jnp.concatenate([tail_cols[p]] * 2, axis=1)
-            lo = lower[128 * p : 128 * p + 128]
-            up = upper[128 * p : 128 * p + 128] + column * last[p : p + 1, :]
-            is_odd = jnp.concatenate([odd[p]] * 2, axis=1)
+            low = jnp.concatenate([t[pl.ds(p, 1024, stride=2), :] for t in table], axis=1)
+            high = jnp.concatenate([t[pl.ds(2048 + p, 1024, stride=2), :] for t in table], axis=1)
+            both = jnp.dot(wide(coef_hi.at[p]), high, preferred_element_type=F32)
+            lo = both[:128] + jnp.dot(wide(coef_lo.at[p]), low, preferred_element_type=F32)
+            column = jnp.concatenate([tail_cols[p]] * 4, axis=1)
+            up = both[128:] + column * last[p : p + 1, :]
+            is_odd = jnp.concatenate([odd[p]] * 4, axis=1)
             even, other = jnp.where(is_odd, up, lo).astype(BF16), jnp.where(is_odd, lo, up).astype(BF16)
-            for b in range(2):
-                spec[2 * q + b, 256 * p : 256 * p + 128, :] = even[:, 128 * b : 128 * b + 128]
-                spec[2 * q + b, 256 * p + 128 : 256 * p + 256, :] = other[:, 128 * b : 128 * b + 128]
-        for j in range(2):
-            fill(2 * q + j)
+            for b in range(4):
+                spec[4 * q + b, 256 * p : 256 * p + 128, :] = even[:, 128 * b : 128 * b + 128]
+                spec[4 * q + b, 256 * p + 128 : 256 * p + 256, :] = other[:, 128 * b : 128 * b + 128]
+        for j in range(4):
+            fill(4 * q + j)
         return carry
 
-    lax.fori_loop(0, 4, synthesize, 0)
+    lax.fori_loop(0, 2, synthesize, 0)
 
     def send_one(g, target):
         pltpu.make_async_remote_copy(
@@ -286,29 +283,26 @@
     return (even + odd).astype(BF16).reshape(4, 64, 256), (even - odd).astype(BF16).reshape(4, 64, 256)
 
 
-def finish_kernel(wave_ref, lhs_ref, basis_ref, energy_in, out_ref, energy_ref, second, sem):
-    first = pltpu.make_async_copy(wave_ref, out_ref.at[0:4], sem.at[0])
-    first.start()
-    energy_ref[...] = energy_in[:, :64]
-
-    def store(k, half):
-        at = pl.ds(pl.multiple_of(k * 512 + HALF * half, 512), 512)
-        return pltpu.make_async_copy(second.at[:, :, at], out_ref.at[4:8, :, at], sem.at[1 + 2 * k + half])
-
-    def stage(k, carry):
-        for j in range(2):
-            low, high = synthesis(lhs_ref, basis_ref, 2 * k + j)
-            second[:, :, pl.ds(pl.multiple_of(k * 512 + 256 * j, 256), 256)] = low
-            second[:, :, pl.ds(pl.multiple_of(k * 512 + 256 * j + HALF, 256), 256)] = high
-        store(k, 0).start()
-        store(k, 1).start()
-        return carry
-
-    lax.fori_loop(0, 4, stage, 0)
-    first.wait()
-    for k in range(4):
-        store(k, 0).wait()
-        store(k, 1).wait()
+def finish_kernel(wave_ref, lhs_ref, basis_ref, energy_in, out_ref, energy_ref, second, energy, sem):
+    energy[...] = energy_in[:, :64]
+    copies = [
+        pltpu.make_async_copy(wave_ref, out_ref.at[0:4], sem.at[0]),
+        pltpu.make_async_copy(energy, energy_ref, sem.at[9]),
+    ]
+    for copy in copies:
+        copy.start()
+    for k in range(HALF // 256):
+        low, high = synthesis(lhs_ref, basis_ref, k)
+        second[:, :, 256 * k : 256 * k + 256] = low
+        second[:, :, HALF + 256 * k : HALF + 256 * k + 256] = high
+        if k % 2 == 1:
+            for j, start in enumerate((256 * (k - 1), HALF + 256 * (k - 1))):
+                at = pl.ds(start, 512)
+                copy = pltpu.make_async_copy(second.at[:, :, at], out_ref.at[4:8, :, at], sem.at[k + j])
+                copy.start()
+                copies.append(copy)
+    for copy in copies:
+        copy.wait()
 
 
 def shards(load_coef, legendre, slab_orders, cycle_rows):
@@ -334,8 +328,8 @@
             pltpu.VMEM((8, 128), jnp.int32),
             pltpu.VMEM((256, 128), F32),
             pltpu.VMEM((8, 1024, 128), BF16),
-            pltpu.VMEM((16, 256, 128), BF16),
-            pltpu.VMEM((16, 512, 128), BF16),
+            pltpu.VMEM((2, 8, 128, 128), BF16),
+            pltpu.VMEM((2, 8, 256, 128), BF16),
             pltpu.VMEM((8, 512, 128), BF16),
             pltpu.VMEM((2, N, 16, 128), BF16),
             pltpu.VMEM((2, N, 16, 128), BF16),
@@ -362,8 +356,12 @@
             jax.ShapeDtypeStruct((1, 64), F32),
         ),
         in_specs=[vmem] * 4,
-        out_specs=(hbm, vmem),
-        scratch_shapes=[pltpu.VMEM((4, 64, NLON), BF16), pltpu.SemaphoreType.DMA((9,))],
+        out_specs=(hbm, hbm),
+        scratch_shapes=[
+            pltpu.VMEM((4, 64, NLON), BF16),
+            pltpu.VMEM((1, 64), F32),
+            pltpu.SemaphoreType.DMA((10,)),
+        ],
         name="finish",
         compiler_params=pltpu.CompilerParams(vmem_limit_bytes=24 * 2**20),
     )(wave, lhs, basis, energy)

time: 45.1 us -> 40.8 us (0.905)
  Pallas kernels: 44.4 us -> 40.1 us
    pallas_call x1, Pallas kernels: 41.1 us -> 38 us  [shards(): pl.pallas_call(exchange_kernel, out_shape=(jax.ShapeDtypeStruct((4, 64, N...]
    pallas_call x1, Pallas kernels: 3.24 us -> 2.14 us  [shards(): pl.pallas_call(finish_kernel, out_shape=(jax.ShapeDtypeStruct((8, 64, NLO...]
where the time goes in v5:
time: 40.8 us
  Pallas kernels  40.1 us (98%)
  between operations  0.64 us (2%)
    pallas_call x1, Pallas kernels, shards(): pl.pallas_call(exchange_kernel, out_shape=(jax.ShapeDtypeStruct((4, 64, N...  38 us
    pallas_call x1, Pallas kernels, shards(): pl.pallas_call(finish_kernel, out_shape=(jax.ShapeDtypeStruct((8, 64, NLO...  2.14 us

profile of v5, /device:TPU:1, one launch (start us, length us, event | category | flops | bytes accessed | tf_op | source)
XLA Modules:
  0.0 40.8 jit_solution(3568840562965759705)
XLA Ops:
  0.6 38.0 %exchange.1 = (bf16[4,64,4096]{2,1,0:T(8,128)(2,1)S(1)}, bf16[2,4,256,128]{3,2,1,0:T(8,128)(2,1)S(1)}, bf16[2,16,512,128]{3,2,1,0:T(8,128)(2,1)S(1)}, f32[1,128]{1,0:T(1,128)S(1)}) custom-call(bf16[2049,8,2,128]{3,2,1,0:T(2,128)(2,1)} %bitcast.7, bf16[2049,2,128]{2,1,0:T(2,128)(2,1)} %bitcast.8, s32[2,128]{1,0:T(2,128)} %bitcast.10, s32[8,128]{1,0:T(8,128)} %bitcast.9), custom_call_target="tpu_custom_call" | custom-call | tf_op jit(solution)/shard_map/exchange/pallas_call | solution.py:314
  38.6 2.1 %finish.1 = (bf16[8,64,4096]{2,1,0:T(8,128)(2,1)}, f32[1,64]{1,0:T(1,128)}) custom-call(bf16[4,64,4096]{2,1,0:T(8,128)(2,1)S(1)} %get-tuple-element.8.wave_ref, bf16[2,4,256,128]{3,2,1,0:T(8,128)(2,1)S(1)} %get-tuple-element.9.lhs_ref, bf16[2,16,512,128]{3,2,1,0:T(8,128)(2,1)S(1)} %get-tuple-element.10.basis_ref, f32[1,128]{1,0:T(1,128)S(1)} %get-tuple-element.11.energy_in), custom_call_target="tpu_custom_call" | custom-call | tf_op jit(solution)/shard_map/finish/pallas_call | solution.py:352

commit v6 on v5

--- a/solution.py
+++ b/solution.py
@@ -212,7 +212,14 @@
 
     for d in range(1, 4):
         send_energy(0, mine_u + 32 * lax.rem(mine_z + d, 4), ecolumn.at[mine_z])
-    to_all(functools.partial(send_one, 1))
+    for d in (2, 3, 1, 0):
+        z = lax.rem(mine_z + d, 4)
+
+        def second_sends(u, carry, z=z):
+            send_one(1, plane(me, u) + 32 * z)
+            return carry
+
+        lax.fori_loop(0 if d else 1, 32, second_sends, 0)
     incoming[1, me] = outgoing[1, me]
 
     lane = lanes((128, 128))

time: 40.8 us -> 38.9 us (0.953)
  Pallas kernels: 40.1 us -> 38.2 us
    pallas_call x1, Pallas kernels: 38 us -> 36.1 us  [shards(): pl.pallas_call(exchange_kernel, out_shape=(jax.ShapeDtypeStruct((4, 64, N...]
where the time goes in v6:
time: 38.9 us; the launch traced here: 38.8 us
  Pallas kernels  38.2 us (98%)
  between operations  0.64 us (2%)
    pallas_call x1, Pallas kernels, shards(): pl.pallas_call(exchange_kernel, out_shape=(jax.ShapeDtypeStruct((4, 64, N...  36.1 us
    pallas_call x1, Pallas kernels, shards(): pl.pallas_call(finish_kernel, out_shape=(jax.ShapeDtypeStruct((8, 64, NLO...  2.14 us

profile of v6, /device:TPU:1, one launch (start us, length us, event | category | flops | bytes accessed | tf_op | source)
XLA Modules:
  0.0 38.8 jit_solution(1373680945363805917)
XLA Ops:
  0.6 36.1 %exchange.1 = (bf16[4,64,4096]{2,1,0:T(8,128)(2,1)S(1)}, bf16[2,4,256,128]{3,2,1,0:T(8,128)(2,1)S(1)}, bf16[2,16,512,128]{3,2,1,0:T(8,128)(2,1)S(1)}, f32[1,128]{1,0:T(1,128)S(1)}) custom-call(bf16[2049,8,2,128]{3,2,1,0:T(2,128)(2,1)} %bitcast.7, bf16[2049,2,128]{2,1,0:T(2,128)(2,1)} %bitcast.8, s32[2,128]{1,0:T(2,128)} %bitcast.10, s32[8,128]{1,0:T(8,128)} %bitcast.9), custom_call_target="tpu_custom_call" | custom-call | tf_op jit(solution)/shard_map/exchange/pallas_call | solution.py:321
  36.7 2.1 %finish.1 = (bf16[8,64,4096]{2,1,0:T(8,128)(2,1)}, f32[1,64]{1,0:T(1,128)}) custom-call(bf16[4,64,4096]{2,1,0:T(8,128)(2,1)S(1)} %get-tuple-element.8.wave_ref, bf16[2,4,256,128]{3,2,1,0:T(8,128)(2,1)S(1)} %get-tuple-element.9.lhs_ref, bf16[2,16,512,128]{3,2,1,0:T(8,128)(2,1)S(1)} %get-tuple-element.10.basis_ref, f32[1,128]{1,0:T(1,128)S(1)} %get-tuple-element.11.energy_in), custom_call_target="tpu_custom_call" | custom-call | tf_op jit(solution)/shard_map/finish/pallas_call | solution.py:359
